TPU v7x, 32 devices: a whole 2x2x4 slice. The times are simulated.
32 devices in a mesh: kpt: 2 (over x), grid: 16 (over z, y, core).
Axes of the slice: x: 2, y: 2, z: 4, core: 2. Of those that a mesh axis runs over, the one named last changes fastest.
Arguments:
- orbitals: bfloat16 [4, 2, 2, 512, 256, 256], P('kpt', None, None, 'grid'), may hold values from -6 to 6
- kweights: int32 [4], P('kpt'), may hold values from 1 to 16
- occupations: int32 [4, 2], P('kpt'), may hold values from 0 to 2
- z_basis: float32 [512, 512], replicated, may hold values from -0.25 to 0.25
- z_eigen: float32 [512], replicated, may hold values from 0.25 to 4
Outputs:
- potential: float32 [512, 256, 256], P('grid')
All inputs are finite; a program needn't handle non-finite values.
Results may differ from a plain program's by a relative error of at most 0.0003.
Values sent between devices are 32-bit elements; how exact they have to be, the bound alone decides.
No kernel may reach another device: no remote copies, remote signals or barrier semaphores. Data moves between devices by JAX's collectives and lax.ppermute only.
A program may use at most 128 MiB of HBM per device.

v0:
```python
from functools import partial

import jax
import jax.numpy as jnp
from jax import lax
from jax.sharding import PartitionSpec as P

precise = lax.Precision.HIGHEST


def real_basis(length):
    position = jnp.arange(length, dtype=jnp.int32)
    product = position[:, None] * position[None, :] % length
    angles = product.astype(jnp.float32) * (2.0 * jnp.pi / length)
    lower = position[:, None] <= length // 2
    table = jnp.where(lower, jnp.cos(angles), jnp.sin(angles))
    edges = (position == 0) | (position == length // 2)
    weights = jnp.where(edges, 1.0, 2.0).astype(jnp.float32) / length
    return (table, table * weights[:, None])


def forward_real(density, bases):
    table_x, scaled_x, table_y, scaled_y = bases
    along = jnp.einsum("zxy,ky->zxk", density, table_y, precision=precise)
    return jnp.einsum("jx,zxk->zjk", table_x, along, precision=precise)[None]


def inverse_real(planes, bases):
    table_x, scaled_x, table_y, scaled_y = bases
    half_done = jnp.einsum("jx,zjk->zxk", scaled_x, planes[0], precision=precise)
    return jnp.einsum("zxk,ky->zxy", half_done, scaled_y, precision=precise)


def scale_table(z_eigen, kx_start, kx_count, x_length, y_length):
    wave_x = (kx_start + jnp.arange(kx_count, dtype=jnp.int32)).astype(jnp.float32)
    wave_y = jnp.arange(y_length, dtype=jnp.int32).astype(jnp.float32)
    shift_x = 2.0 * jnp.sin(jnp.pi * wave_x / x_length)
    shift_y = 2.0 * jnp.sin(jnp.pi * wave_y / y_length)
    shifted = shift_x[:, None] ** 2 + shift_y[None, :] ** 2
    return 1.0 / (z_eigen[:, None, None] + shifted[None])


def kernel_columns(z_rows, factors, columns):
    projected = jnp.einsum("zj,czab->cjab", z_rows, columns, precision=precise)
    return jnp.einsum("zj,cjab->czab", z_rows, projected * factors[None], precision=precise)


def on_device(orbitals, kweights, occupations, z_basis, z_eigen):
    points = orbitals.shape[0]
    band_count = orbitals.shape[1]
    x_length = orbitals.shape[4]
    y_length = orbitals.shape[5]
    factor = (kweights[:, None] * occupations).astype(jnp.float32) / (16.0 * points * band_count)
    values = orbitals.astype(jnp.float32)
    partial_sum = jnp.sum(factor[:, :, None, None, None, None] * values * values, axis=(0, 1, 2))
    table_x, scaled_x = real_basis(x_length)
    table_y, scaled_y = real_basis(y_length)
    forward = partial(forward_real, bases=(table_x, scaled_x, table_y, scaled_y))
    inverse = partial(inverse_real, bases=(table_x, scaled_x, table_y, scaled_y))
    blocks = lax.axis_size("grid")
    density = lax.psum(partial_sum, "kpt")
    spectrum = forward(density)
    kx_count = x_length // blocks
    kx_start = lax.axis_index("grid") * kx_count
    factors = scale_table(z_eigen, kx_start, kx_count, x_length, y_length)
    columns = kernel_columns(
        z_basis, factors, lax.all_to_all(spectrum, "grid", split_axis=2, concat_axis=1, tiled=True)
    )
    planes = lax.all_to_all(columns, "grid", split_axis=1, concat_axis=2, tiled=True)
    potential = inverse(planes)
    return potential


def solution(mesh):
    return jax.shard_map(
        on_device,
        mesh=mesh,
        in_specs=(P("kpt", None, None, "grid", None, None), P("kpt"), P("kpt", None), P(), P()),
        out_specs=P("grid", None, None),
        check_vma=False,
    )
```

profile of v0, /device:TPU:13, one launch (start us, length us, event | category | flops | bytes accessed | tf_op | source)
XLA Modules:
  0.0 750.4 jit_solution(17960610065291599581)
XLA Ops:
  6.5 0.0 copy-start
  6.5 0.0 all-reduce.2.cloned.1.call-start
  6.5 0.8 convert_multiply_fusion
  7.4 18.9 %fusion = f32[32,256,256]{2,1,0:T(8,128)} fusion(bf16[2,2,2,32,256,256]{5,4,3,2,1,0:T(8,128)(2,1)} %param.5, f32[2,2]{1,0:T(2,128)S(1)} %convert_multiply_fusion), kind=kLoop, calls=%fused_computation.1 | loop fusion | flops 65011712 | bytes 41943056 | tf_op jit(solution)/shard_map/reduce_sum | solution.py:55
  26.3 0.0 all-reduce.2.cloned.1.call-update
  26.4 199.1 %all-reduce.2.cloned.1.call-done = f32[32,256,256]{2,1,0:T(8,128)} async-done(((f32[32,256,256]{2,1,0:T(8,128)}), f32[32,256,256]{2,1,0:T(8,128)}) %all-reduce.2.cloned.1.call-update) | async-done | bytes 8388624 | tf_op jit(solution)/shard_map/psum | solution.py:61
  225.5 12.7 %fusion.25 = f32[32,256,256]{1,2,0:T(8,128)S(1)} fusion(f32[32,256,256]{2,1,0:T(8,128)} %all-reduce.2.cloned.1.call-done, pred[256]{0:T(512)(128)(4,1)S(1)} %iota_compare_fusion), kind=kOutput, calls=%fused_computation.28 | convolution fusion | flops 6443433984 | bytes 16777472 | tf_op jit(solution)/shard_map/zxy,ky->zxk/dot_general | solution.py:24
  238.2 23.2 %convolution_bitcast_fusion = f32[1,32,256,256]{2,3,1,0:T(8,128)} fusion(f32[32,256,256]{1,2,0:T(8,128)S(1)} %fusion.25, pred[256]{0:T(512)(128)(4,1)S(1)} %iota_compare_fusion), kind=kOutput, calls=%fused_computation.14 | convolution fusion | flops 6443433984 | bytes 16777472 | tf_op jit(solution)/shard_map/jx,zxk->zjk/dot_general | solution.py:25
  261.4 10.3 %copy.13 = f32[1,32,256,256]{3,1,0,2:T(8,128)} copy(f32[1,32,256,256]{2,3,1,0:T(8,128)} %convolution_bitcast_fusion) | data formatting | bytes 16777216 | tf_op jit(solution)/shard_map/broadcast_in_dim | solution.py:25
  271.7 6.5 all-to-all-start
  278.3 0.1 broadcast_add_fusion
  278.4 182.2 %all-to-all-done = f32[1,32,256,256]{3,1,0,2:T(8,128)} async-done(((f32[1,32,256,256]{3,1,0,2:T(8,128)}), f32[1,32,256,256]{3,1,0,2:T(8,128)}, u32[]{:S(2)}, u32[]{:S(2)}) %all-to-all-start) | async-done | bytes 8388640 | tf_op jit(solution)/shard_map/all_to_all | solution.py:67
  460.6 8.2 %copy.14 = f32[1,32,256,256]{3,2,1,0:T(8,128)S(1)} copy(f32[1,32,256,256]{3,1,0,2:T(8,128)} %all-to-all-done) | data formatting | bytes 16777216 | tf_op jit(solution)/shard_map/all_to_all | solution.py:67
  468.8 1.4 copy.15
  470.2 0.0 copy-done
  470.2 0.0 copy-start.2
  470.2 21.4 %fusion.6 = f32[16,256,512]{2,1,0:T(8,128)S(1)} fusion(f32[512,16,256]{2,1,0:T(8,128)S(1)} %bitcast.51, f32[512,512]{1,0:T(8,128)S(1)} %copy-done), kind=kOutput, calls=%fused_computation.7 | convolution fusion | flops 12884901888 | bytes 17825792 | tf_op jit(solution)/shard_map/zj,czab->cjab/dot_general | solution.py:44
  491.7 0.0 copy-done.2
  491.7 16.4 %fusion.13 = f32[1,512,16,256]{1,3,2,0:T(8,128)} fusion(f32[16,256,512]{2,1,0:T(8,128)S(1)} %fusion.6, f32[16,256]{1,0:T(8,128)S(1)} %broadcast_add_fusion, f32[512]{0:T(512)S(1)} %copy-done.2, f32[512,512]{1,0:T(8,128)S(1)} %copy-done), kind=kOutput, calls=%fused_computation.15 | convolution fusion | flops 12891193344 | bytes 17844224 | tf_op jit(solution)/shard_map/zj,cjab->czab/dot_general | solution.py:45
  508.1 10.3 %copy.17 = f32[1,512,16,256]{3,2,0,1:T(8,128)} copy(f32[1,512,16,256]{1,3,2,0:T(8,128)} %fusion.13) | data formatting | bytes 16777216 | tf_op jit(solution)/shard_map/zj,cjab->czab/transpose | solution.py:45
  518.3 5.0 all-to-all-start.1
  523.3 182.1 %all-to-all-done.1 = f32[1,512,16,256]{3,2,0,1:T(8,128)} async-done(((f32[1,512,16,256]{3,2,0,1:T(8,128)}), f32[1,512,16,256]{3,2,0,1:T(8,128)}, u32[]{:S(2)}, u32[]{:S(2)}) %all-to-all-start.1) | async-done | bytes 8388640 | tf_op jit(solution)/shard_map/all_to_all | solution.py:69
  705.5 4.4 copy.18
  709.8 0.0 copy-start.1
  709.8 15.4 %fusion.22 = f32[32,256,256]{2,1,0:T(8,128)S(1)} fusion(f32[32,256,256]{2,1,0:T(8,128)S(1)} %bitcast.52, f32[256]{0:T(256)S(1)} %fusion.34, pred[256]{0:T(512)(128)(4,1)S(1)} %iota_compare_fusion), kind=kOutput, calls=%fused_computation.25 | convolution fusion | flops 6443499520 | bytes 16778496 | tf_op jit(solution)/shard_map/jx,zjk->zxk/dot_general | solution.py:30
  725.3 17.9 %fusion.4 = f32[32,256,256]{2,1,0:T(8,128)} fusion(f32[32,256,256]{2,1,0:T(8,128)S(1)} %fusion.22, f32[256]{0:T(256)S(1)} %fusion.34, pred[256]{0:T(512)(128)(4,1)S(1)} %iota_compare_fusion), kind=kOutput, calls=%fused_computation.5 | convolution fusion | flops 6443499520 | bytes 16778496 | tf_op jit(solution)/shard_map/zxk,ky->zxy/dot_general | solution.py:31
  743.2 0.0 copy-done.1
  (4 shorter events, 0.1 us)
Async XLA Ops:
  6.5 463.7 %copy-start = (f32[512,512]{1,0:T(8,128)S(1)}, f32[512,512]{1,0:T(8,128)}, u32[]{:S(2)}) copy-start(f32[512,512]{1,0:T(8,128)} %param.8) | copy-start | bytes 3145732
  6.5 219.0 %all-reduce.2.cloned.1.call-start = ((), (), s32[]{:S(2)}) async-start(), calls=%async_computation.2 | async-start | bytes 16777216 | tf_op jit(solution)/shard_map/psum | solution.py:61
  271.7 188.9 %all-to-all-start = ((f32[1,32,256,256]{3,1,0,2:T(8,128)}), f32[1,32,256,256]{3,1,0,2:T(8,128)}, u32[]{:S(2)}, u32[]{:S(2)}) async-start(f32[1,32,256,256]{3,1,0,2:T(8,128)} %copy.13), calls=%async_computation | async-start | bytes 16777216 | tf_op jit(solution)/shard_map/all_to_all | solution.py:67
  470.2 21.4 %copy-start.2 = (f32[512]{0:T(512)S(1)}, f32[512]{0:T(512)}, u32[]{:S(2)}) copy-start(f32[512]{0:T(512)} %param.9) | copy-start | bytes 6148
  518.3 187.1 %all-to-all-start.1 = ((f32[1,512,16,256]{3,2,0,1:T(8,128)}), f32[1,512,16,256]{3,2,0,1:T(8,128)}, u32[]{:S(2)}, u32[]{:S(2)}) async-start(f32[1,512,16,256]{3,2,0,1:T(8,128)} %copy.17), calls=%async_computation.1 | async-start | bytes 16777216 | tf_op jit(solution)/shard_map/all_to_all | solution.py:69
  709.8 33.3 %copy-start.1 = (f32[512,512]{1,0:T(8,128)S(1)}, f32[512,512]{1,0:T(8,128)}, u32[]{:S(2)}) copy-start(f32[512,512]{1,0:T(8,128)} %param.8) | copy-start | bytes 3145732
Sparse Core Ops, SparseCore 0:
  26.5 198.9 all-reduce.1
where the time goes:
time: 757 us; the launch traced here: 750 us
  waiting for transfers between devices  563 us (74%)
  matrix products  107 us (14%)
  local copies, waits for them, and re-layouts  34.6 us (5%)
  other arithmetic  20 us (3%)
  between operations  13.9 us (2%)
  starting transfers between devices  11.5 us (2%)
    psum x1, waiting for transfers between devices, on_device(): density = lax.psum(partial_sum, 'kpt')  199 us
    all_to_all x1, waiting for transfers between devices, on_device(): lax.all_to_all(spectrum, 'grid', split_axis=2, concat_axis=1, tiled=True)  182 us
    all_to_all x1, waiting for transfers between devices, on_device(): lax.all_to_all(columns, 'grid', split_axis=1, concat_axis=2, tiled=True)  182 us
    dot_general x1, matrix products, forward_real(): return jnp.einsum('jx,zxk->zjk', table_x, along, precision=precise)[None]  23.2 us
    dot_general x1, matrix products, kernel_columns(): projected = jnp.einsum('zj,czab->cjab', z_rows, columns, precision=precise)  21.4 us
    reduce_sum x1, other arithmetic, on_device(): jnp.sum(factor[:, :, None, None, None, None] * values * values, axis=(0,...  18.9 us
    dot_general x1, matrix products, inverse_real(): return jnp.einsum('zxk,ky->zxy', half_done, scaled_y, precision=precise)  17.9 us
    dot_general x1, matrix products, kernel_columns(): jnp.einsum('zj,cjab->czab', z_rows, projected * factors[None], precision=...  16.4 us
  transfers between devices with their start and end apart: 3, of which 3 were waited for; matrix products, arithmetic and copies ran while one was open for 0% of the time, Pallas kernels for 0%

commit v1 on v0

v1 whole, which is shorter than its diff:
```python
import numpy as np
import jax
import jax.numpy as jnp
from jax import lax
from jax.experimental import pallas as pl
from jax.experimental.pallas import tpu as pltpu
from jax.sharding import PartitionSpec as P


f32 = jnp.float32
bf16 = jnp.bfloat16


def real_basis(length):
    position = np.arange(length)
    angles = (position[:, None] * position[None, :] % length) * (2.0 * np.pi / length)
    table = np.where(position[:, None] <= length // 2, np.cos(angles), np.sin(angles))
    edges = (position == 0) | (position == length // 2)
    weights = np.where(edges, 1.0, 2.0) / length
    return table.astype(np.float32), (table * weights[:, None]).astype(np.float32)


def split_const(table):
    high = table.astype(jnp.bfloat16)
    low = (table - high.astype(np.float32)).astype(jnp.bfloat16)
    return jnp.asarray(high), jnp.asarray(low)


def split(value):
    high = value.astype(bf16)
    return high, (value - high.astype(f32)).astype(bf16)


def dot3(ah, al, bh, bl):
    def one(a, b):
        return jnp.dot(a, b, preferred_element_type=f32)

    return one(ah, bh) + (one(ah, bl) + one(al, bh))


def whole(shape):
    zeros = (0,) * len(shape)
    return pl.BlockSpec(shape, lambda *_: zeros)


def smem():
    return pl.BlockSpec(memory_space=pltpu.SMEM)


def cost(flops, bytes_accessed):
    return pl.CostEstimate(flops=int(flops), bytes_accessed=int(bytes_accessed), transcendentals=0)


GROUP = 8


def forward(orbitals, kweights, occupations, half, tables, chunk, blocks, step=2):
    points, bands, parts, _, nx, ny = orbitals.shape
    rows = nx // (2 * blocks)
    steps = GROUP // step
    scale = 1.0 / (16.0 * points * bands)

    def body(half_ref, kweights_ref, occ_ref, orb_ref, yh_ref, yl_ref, xh_ref, xl_ref, own_ref, other_ref, s_ref):
        mine = half_ref[0]
        here = pl.program_id(0)
        yh, yl = yh_ref[...], yl_ref[...]
        for plane in range(step):
            total = None
            for point in range(points):
                for band in range(bands):
                    weight = (kweights_ref[point] * occ_ref[point, band]).astype(f32) * scale
                    real = orb_ref[point, band, 0, plane].astype(f32)
                    imag = orb_ref[point, band, 1, plane].astype(f32)
                    term = weight * (real * real + imag * imag)
                    total = term if total is None else total + term
            dh, dl = split(total)
            ah, al = split(dot3(dh, dl, yh, yl))
            s_ref[here * step + plane] = dot3(xh_ref[...], xl_ref[...], ah, al)

        @pl.when(here == steps - 1)
        def _():
            for slot, out in ((0, own_ref), (1, other_ref)):
                first = pl.multiple_of((mine if slot == 0 else 1 - mine) * (nx // 2), nx // 2)
                for plane in range(GROUP):
                    out[:, :, plane, :] = s_ref[plane, pl.ds(first, nx // 2), :].reshape(blocks, rows, ny)

    out_shape = jax.ShapeDtypeStruct((blocks, rows, GROUP, ny), f32)
    return pl.pallas_call(
        body,
        grid=(steps,),
        in_specs=[smem(), smem(), smem()]
        + [pl.BlockSpec((points, bands, parts, step, nx, ny), lambda i: (0, 0, 0, chunk * steps + i, 0, 0))]
        + [whole(t.shape) for t in tables],
        out_specs=[whole(out_shape.shape)] * 2,
        out_shape=[out_shape] * 2,
        scratch_shapes=[pltpu.VMEM((GROUP, nx, ny), f32)],
        cost_estimate=cost(GROUP * 12 * nx * ny * nx, GROUP * nx * ny * 24),
        name="forward",
    )(half, kweights, occupations, orbitals, *tables)


def prepare(z_basis, blocks, planes):
    nz = z_basis.shape[0]
    chunks = planes // GROUP
    size = blocks * GROUP

    def body(z_ref, zh_ref, zl_ref, th_ref, tl_ref):
        value = z_ref[...].reshape(size, nz)
        zh_ref[0], zl_ref[0] = split(value)
        th_ref[0], tl_ref[0] = split(value.T)

    straight = jax.ShapeDtypeStruct((chunks, size, nz), bf16)
    turned = jax.ShapeDtypeStruct((chunks, nz, size), bf16)
    return pl.pallas_call(
        body,
        grid=(chunks,),
        in_specs=[pl.BlockSpec((blocks, GROUP, nz), lambda i: (0, i, 0))],
        out_specs=[pl.BlockSpec((1, size, nz), lambda i: (i, 0, 0))] * 2 + [pl.BlockSpec((1, nz, size), lambda i: (i, 0, 0))] * 2,
        out_shape=[straight] * 2 + [turned] * 2,
        cost_estimate=cost(nz * nz * 100, nz * nz * 12),
        name="prepare",
    )(z_basis.reshape(blocks, planes, nz))


def by_row(blocks, ny):
    return pl.BlockSpec((blocks, 1, GROUP, ny), lambda i: (0, i, 0, 0))


def one_chunk(table, chunk):
    return pl.BlockSpec((1,) + table.shape[1:], lambda i: (chunk, 0, 0))


def project(columns, turned, chunk, before):
    blocks, rows, _, ny = columns.shape
    nz = turned[0].shape[1]
    size = blocks * GROUP
    extra = () if before is None else (before,)

    def body(x_ref, th_ref, tl_ref, *refs):
        xh, xl = split(x_ref[:, 0].reshape(size, ny))
        value = dot3(th_ref[0], tl_ref[0], xh, xl)
        refs[-1][0] = value if before is None else value + refs[0][0]

    part = pl.BlockSpec((1, nz, ny), lambda i: (i, 0, 0))
    return pl.pallas_call(
        body,
        grid=(rows,),
        in_specs=[by_row(blocks, ny)] + [one_chunk(t, chunk) for t in turned] + [part for _ in extra],
        out_specs=part,
        out_shape=jax.ShapeDtypeStruct((rows, nz, ny), f32),
        cost_estimate=cost(6 * nz * size * rows * ny, 8 * nz * rows * ny),
        name="project",
    )(columns, *turned, *extra)


def solve(part, columns, straight, turned, eigen, shift, chunk):
    blocks, rows, _, ny = columns.shape
    nz = turned[0].shape[1]
    size = blocks * GROUP

    def body(part_ref, x_ref, th_ref, tl_ref, zh_ref, zl_ref, e_ref, s_ref, out_ref, wh_ref, wl_ref):
        xh, xl = split(x_ref[:, 0].reshape(size, ny))
        projected = part_ref[0] + dot3(th_ref[0], tl_ref[0], xh, xl)
        wh, wl = split(projected / (e_ref[...] + s_ref[0]))
        wh_ref[0], wl_ref[0] = wh, wl
        out_ref[:, 0] = dot3(zh_ref[0], zl_ref[0], wh, wl).reshape(blocks, GROUP, ny)

    w_spec = pl.BlockSpec((1, nz, ny), lambda i: (i, 0, 0))
    w_shape = jax.ShapeDtypeStruct((rows, nz, ny), bf16)
    return pl.pallas_call(
        body,
        grid=(rows,),
        in_specs=[w_spec, by_row(blocks, ny)]
        + [one_chunk(t, chunk) for t in turned]
        + [one_chunk(z, 0) for z in straight]
        + [whole(eigen.shape), pl.BlockSpec((1, 1, ny), lambda i: (i, 0, 0))],
        out_specs=[by_row(blocks, ny), w_spec, w_spec],
        out_shape=[jax.ShapeDtypeStruct(columns.shape, f32), w_shape, w_shape],
        cost_estimate=cost(12 * nz * rows * ny * size, 12 * nz * rows * ny),
        name="solve",
    )(part, columns, *turned, *straight, eigen, shift)


def filtered(wh, wl, straight, chunk, blocks):
    rows, nz, ny = wh.shape

    def body(wh_ref, wl_ref, zh_ref, zl_ref, out_ref):
        out_ref[:, 0] = dot3(zh_ref[0], zl_ref[0], wh_ref[0], wl_ref[0]).reshape(blocks, GROUP, ny)

    w_spec = pl.BlockSpec((1, nz, ny), lambda i: (i, 0, 0))
    return pl.pallas_call(
        body,
        grid=(rows,),
        in_specs=[w_spec, w_spec] + [one_chunk(z, chunk) for z in straight],
        out_specs=by_row(blocks, ny),
        out_shape=jax.ShapeDtypeStruct((blocks, rows, GROUP, ny), f32),
        cost_estimate=cost(6 * nz * rows * ny * blocks * GROUP, 4 * nz * rows * ny),
        name="filtered",
    )(wh, wl, *straight)


def inverse(own, other, half, tables, planes, chunk, into, step=2):
    blocks, rows, _, ny = own.shape
    nx = 2 * blocks * rows
    steps = GROUP // step
    extra = () if into is None else (into,)

    def body(half_ref, own_ref, other_ref, yh_ref, yl_ref, xh_ref, xl_ref, *refs):
        out_ref, f_ref = refs[-2:]
        here = pl.program_id(0)

        @pl.when(here == 0)
        def _():
            for slot, ref in ((0, own_ref), (1, other_ref)):
                first = pl.multiple_of((half_ref[0] if slot == 0 else 1 - half_ref[0]) * (nx // 2), nx // 2)
                for plane in range(GROUP):
                    f_ref[plane, pl.ds(first, nx // 2), :] = ref[:, :, plane, :].reshape(nx // 2, ny)

        for plane in range(step):
            fh, fl = split(f_ref[here * step + plane])
            hh, hl = split(dot3(fh, fl, yh_ref[...], yl_ref[...]))
            out_ref[plane] = dot3(xh_ref[...], xl_ref[...], hh, hl)

    operands = (half, own, other, *tables, *extra)
    return pl.pallas_call(
        body,
        grid=(steps,),
        in_specs=[smem(), whole(own.shape), whole(other.shape)]
        + [whole(t.shape) for t in tables]
        + [pl.BlockSpec(memory_space=pl.ANY) for _ in extra],
        out_specs=pl.BlockSpec((step, nx, ny), lambda i: (chunk * steps + i, 0, 0)),
        out_shape=jax.ShapeDtypeStruct((planes, nx, ny), f32),
        scratch_shapes=[pltpu.VMEM((GROUP, nx, ny), f32)],
        input_output_aliases={len(operands) - 1: 0} if extra else {},
        cost_estimate=cost(GROUP * 12 * nx * ny * nx, GROUP * nx * ny * 8),
        name="inverse",
    )(*operands)


def row_shift(first, rows, nx, ny):
    wave_x = (first + jnp.arange(rows, dtype=jnp.int32)).astype(f32)
    wave_y = jnp.arange(ny, dtype=jnp.int32).astype(f32)
    shift_x = 2.0 * jnp.sin(jnp.pi * wave_x / nx)
    shift_y = 2.0 * jnp.sin(jnp.pi * wave_y / ny)
    return shift_x[:, None] ** 2 + shift_y[None, :] ** 2


def swap(value):
    return lax.ppermute(value, "kpt", [(0, 1), (1, 0)])


def exchange(value):
    return lax.all_to_all(value, "grid", split_axis=0, concat_axis=0, tiled=True)


def on_device_kernels(orbitals, kweights, occupations, z_basis, z_eigen):
    planes, nx, ny = orbitals.shape[3:]
    blocks = lax.axis_size("grid")
    rows = nx // (2 * blocks)
    chunks = planes // GROUP
    mine = lax.axis_index("kpt").astype(jnp.int32)
    half = mine.reshape(1)
    table_x, scaled_x = real_basis(nx)
    table_y, scaled_y = real_basis(ny)
    to_modes = (*split_const(np.ascontiguousarray(table_y.T)), *split_const(table_x))
    to_grid = (*split_const(scaled_y), *split_const(np.ascontiguousarray(scaled_x.T)))

    columns = []
    for chunk in range(chunks):
        own, other = forward(orbitals, kweights, occupations, half, to_modes, chunk, blocks)
        if chunk == 0:
            z_basis, z_eigen, own = lax.optimization_barrier((z_basis, z_eigen, own))
        other = swap(other)
        own = own + other
        columns.append(exchange(own))
    zh, zl, th, tl = prepare(z_basis, blocks, planes)
    first = (mine * blocks + lax.axis_index("grid")) * rows
    shift = row_shift(first, rows, nx, ny)[:, None, :]
    part = None
    for chunk in range(chunks - 1):
        part = project(columns[chunk], (th, tl), chunk, part)
    if part is None:
        part = jnp.zeros((rows, planes * blocks, ny), f32)
    ready, wh, wl = solve(part, columns[-1], (zh, zl), (th, tl), z_eigen[:, None], shift, chunks - 1)
    out = None
    for chunk in range(chunks):
        ready = ready if chunk == 0 else filtered(wh, wl, (zh, zl), chunk, blocks)
        own = exchange(ready)
        other = swap(own)
        out = inverse(own, other, half, to_grid, planes, chunk, out)
    return out


precise = lax.Precision.HIGHEST


def on_device_plain(orbitals, kweights, occupations, z_basis, z_eigen):
    points, bands, _, planes, nx, ny = orbitals.shape
    blocks = lax.axis_size("grid")
    rows = nx // (2 * blocks)
    nz = planes * blocks
    mine = lax.axis_index("kpt")
    weights = (kweights[:, None] * occupations).astype(f32) / (16.0 * points * bands)
    values = orbitals.astype(f32)
    density = jnp.sum(weights[:, :, None, None, None, None] * values * values, axis=(0, 1, 2))
    table_x, scaled_x = (jnp.roll(jnp.asarray(t), -mine * (nx // 2), axis=0) for t in real_basis(nx))
    table_y, scaled_y = real_basis(ny)
    along = jnp.einsum("zxy,ky->zxk", density, table_y, precision=precise)
    spectrum = jnp.einsum("jx,zxk->jzk", table_x, along, precision=precise).reshape(2, blocks, rows, planes, ny)
    columns = exchange(spectrum[0] + swap(spectrum[1]))
    first = (mine * blocks + lax.axis_index("grid")) * rows
    factors = 1.0 / (z_eigen[:, None, None] + row_shift(first, rows, nx, ny)[None])
    by_plane = z_basis.reshape(blocks, planes, nz)
    projected = jnp.einsum("gpj,gapk->jak", by_plane, columns, precision=precise)
    filtered = jnp.einsum("gpj,jak->gapk", by_plane, projected * factors, precision=precise)
    own = exchange(filtered)
    modes = jnp.stack([own, swap(own)]).reshape(nx, planes, ny)
    half_done = jnp.einsum("jx,jzk->zxk", scaled_x, modes, precision=precise)
    return jnp.einsum("zxk,ky->zxy", half_done, scaled_y, precision=precise)


def whole_tiles(shape, blocks):
    planes, nx, ny = shape[3:]
    rows = nx // (2 * blocks)
    return rows % 8 == 0 and ny % 128 == 0 and nx % 256 == 0 and planes % GROUP == 0


def on_device(orbitals, *rest):
    if not whole_tiles(orbitals.shape, lax.axis_size("grid")):
        return on_device_plain(orbitals, *rest)
    return on_device_kernels(orbitals, *rest)


def solution(mesh):
    step = jax.shard_map(
        on_device,
        mesh=mesh,
        in_specs=(P("kpt", None, None, "grid", None, None), P("kpt"), P("kpt", None), P(), P()),
        out_specs=P("grid", None, None),
        check_vma=False,
    )

    def run(orbitals, *rest):
        blocks = mesh.shape["grid"]
        local = list(orbitals.shape)
        local[3] //= blocks
        if not whole_tiles(local, blocks):
            return step(orbitals, *rest)
        return step(orbitals, *rest)

    return run
```

time: 757 us -> 410 us (0.54)
  waiting for transfers between devices: 563 us -> 215 us
  Pallas kernels: 0 us -> 120 us
  matrix products: 107 us -> 0 us
  starting transfers between devices: 11.5 us -> 57.4 us
  local copies, waits for them, and re-layouts: 34.6 us -> 2.89 us
  between operations: 13.9 us -> 0.05 us
  other arithmetic: 20 us -> 10.1 us
    all_to_all x2 -> x8, waiting for transfers between devices: 364 us -> 76.6 us  [exchange(): lax.all_to_all(value, 'grid', split_axis=0, concat_axis=0, tiled=True)]
    psum x1 -> x0, waiting for transfers between devices: 199 us -> none  [on_device(): density = lax.psum(partial_sum, 'kpt')]
    ppermute x0 -> x8, waiting for transfers between devices: none -> 138 us  [swap(): return lax.ppermute(value, 'kpt', [(0, 1), (1, 0)])]
    pallas_call x0 -> x16, Pallas kernels: none -> 120 us  [the longest x4 35.9 us: forward(): pl.pallas_call(body, grid=(steps,), in_specs=[smem(), smem(), smem()] + [...]
    dot_general x6 -> x0, matrix products: 107 us -> none  [the longest x1 23.2 us: forward_real(): return jnp.einsum('jx,zxk->zjk', table_x, along, precision=precise)[None]]
    all_to_all x2 -> x8, starting transfers between devices: 11.5 us -> 48.7 us  [exchange(): lax.all_to_all(value, 'grid', split_axis=0, concat_axis=0, tiled=True)]
    reduce_sum x1 -> x0, other arithmetic: 18.9 us -> none  [on_device(): jnp.sum(factor[:, :, None, None, None, None] * values * values, axis=(0,...]
    all_to_all x3 -> x0, local copies, waits for them, and re-layouts: 14 us -> none  [the longest x2 9.66 us: on_device(): lax.all_to_all(spectrum, 'grid', split_axis=2, concat_axis=1, tiled=True)]
  transfers between devices with their start and end apart: 3 -> 16, of which waited for: 3 -> 11; matrix products, arithmetic and copies ran while one was open for 0% -> 2% of each run, Pallas kernels for 0% -> 23%
where the time goes in v1:
time: 410 us; the launch traced here: 405 us
  waiting for transfers between devices  215 us (52%)
  Pallas kernels  120 us (29%)
  starting transfers between devices  57.4 us (14%)
  other arithmetic  10.1 us (2%)
    ppermute x8, waiting for transfers between devices, swap(): return lax.ppermute(value, 'kpt', [(0, 1), (1, 0)])  138 us
    all_to_all x8, waiting for transfers between devices, exchange(): lax.all_to_all(value, 'grid', split_axis=0, concat_axis=0, tiled=True)  76.6 us
    all_to_all x8, starting transfers between devices, exchange(): lax.all_to_all(value, 'grid', split_axis=0, concat_axis=0, tiled=True)  48.7 us
    pallas_call x4, Pallas kernels, forward(): pl.pallas_call(body, grid=(steps,), in_specs=[smem(), smem(), smem()] + [...  35.9 us
    pallas_call x4, Pallas kernels, inverse(): pl.pallas_call(body, grid=(steps,), in_specs=[smem(), whole(own.shape), w...  26.8 us
    pallas_call x3, Pallas kernels, project(): pl.pallas_call(body, grid=(rows,), in_specs=[by_row(blocks, ny)] + [one_c...  23.3 us
    pallas_call x3, Pallas kernels, filtered(): pl.pallas_call(body, grid=(rows,), in_specs=[w_spec, w_spec] + [one_chunk...  20.5 us
    pallas_call x1, Pallas kernels, solve(): pl.pallas_call(body, grid=(rows,), in_specs=[w_spec, by_row(blocks, ny)]...  9.37 us
  transfers between devices with their start and end apart: 16, of which 11 were waited for; matrix products, arithmetic and copies ran while one was open for 2% of the time, Pallas kernels for 23%

profile of v1, /device:TPU:13, one launch (start us, length us, event | category | flops | bytes accessed | tf_op | source)
XLA Modules:
  0.0 405.1 jit_solution(15527043454668637339)
XLA Ops:
  0.0 8.9 %forward.5 = (f32[16,8,8,256]{3,2,1,0:T(8,128)}, f32[16,8,8,256]{3,2,1,0:T(8,128)}) custom-call(s32[1]{0:T(128)} %bitcast.half_ref, s32[2]{0:T(128)} %kweights_ref.7, s32[2,2]{1,0:T(2,128)} %occ_ref.7, bf16[2,2,2,32,256,256]{5,4,3,2,1,0:T(8,128)(2,1)} %orb_ref.7, bf16[256,256]{1,0:T(8,128)(2,1)} %constant.41.clone.yh_ref, ...), custom_call_target="tpu_custom_call" | custom-call | flops 1610612736 | bytes 12582912 | tf_op jit(solution)/shard_map/forward/pallas_call | solution.py:88
  10.2 23.0 %collective-permute-done.2 = f32[16,8,8,256]{3,2,1,0:T(8,128)S(1)} collective-permute-done((f32[16,8,8,256]{3,2,1,0:T(8,128)}, f32[16,8,8,256]{3,2,1,0:T(8,128)S(1)}, u32[]{:S(2)}, u32[]{:S(2)}) %collective-permute-start.2) | collective-permute-done | bytes 1048608 | tf_op jit(solution)/shard_map/ppermute | solution.py:249
  35.5 7.4 %all-to-all-start.2 = ((f32[16,8,8,256]{3,2,1,0:T(8,128)}), f32[16,8,8,256]{3,2,1,0:T(8,128)S(1)}, u32[]{:S(2)}, u32[]{:S(2)}) async-start(f32[16,8,8,256]{3,2,1,0:T(8,128)} %add.47), calls=%async_computation.2 | async-start | bytes 2097152 | tf_op jit(solution)/shard_map/all_to_all | solution.py:253
  42.9 9.0 %forward.4 = (f32[16,8,8,256]{3,2,1,0:T(8,128)}, f32[16,8,8,256]{3,2,1,0:T(8,128)}) custom-call(s32[1]{0:T(128)} %bitcast.half_ref, s32[2]{0:T(128)} %kweights_ref.7, s32[2,2]{1,0:T(2,128)} %occ_ref.7, bf16[2,2,2,32,256,256]{5,4,3,2,1,0:T(8,128)(2,1)} %orb_ref.7, bf16[256,256]{1,0:T(8,128)(2,1)} %constant.41.clone.yh_ref, ...), custom_call_target="tpu_custom_call" | custom-call | flops 1610612736 | bytes 12582912 | tf_op jit(solution)/shard_map/forward/pallas_call | solution.py:88
  53.1 23.3 %collective-permute-done = f32[16,8,8,256]{3,2,1,0:T(8,128)S(1)} collective-permute-done((f32[16,8,8,256]{3,2,1,0:T(8,128)}, f32[16,8,8,256]{3,2,1,0:T(8,128)S(1)}, u32[]{:S(2)}, u32[]{:S(2)}) %collective-permute-start) | collective-permute-done | bytes 1048608 | tf_op jit(solution)/shard_map/ppermute | solution.py:249
  78.8 6.9 %all-to-all-start = ((f32[16,8,8,256]{3,2,1,0:T(8,128)}), f32[16,8,8,256]{3,2,1,0:T(8,128)S(1)}, u32[]{:S(2)}, u32[]{:S(2)}) async-start(f32[16,8,8,256]{3,2,1,0:T(8,128)} %add.45), calls=%async_computation | async-start | bytes 2097152 | tf_op jit(solution)/shard_map/all_to_all | solution.py:253
  85.6 9.0 %forward.6 = (f32[16,8,8,256]{3,2,1,0:T(8,128)}, f32[16,8,8,256]{3,2,1,0:T(8,128)}) custom-call(s32[1]{0:T(128)} %bitcast.half_ref, s32[2]{0:T(128)} %kweights_ref.7, s32[2,2]{1,0:T(2,128)} %occ_ref.7, bf16[2,2,2,32,256,256]{5,4,3,2,1,0:T(8,128)(2,1)} %orb_ref.7, bf16[256,256]{1,0:T(8,128)(2,1)} %constant.41.clone.yh_ref, ...), custom_call_target="tpu_custom_call" | custom-call | flops 1610612736 | bytes 12582912 | tf_op jit(solution)/shard_map/forward/pallas_call | solution.py:88
  95.8 23.3 %collective-permute-done.1 = f32[16,8,8,256]{3,2,1,0:T(8,128)S(1)} collective-permute-done((f32[16,8,8,256]{3,2,1,0:T(8,128)}, f32[16,8,8,256]{3,2,1,0:T(8,128)S(1)}, u32[]{:S(2)}, u32[]{:S(2)}) %collective-permute-start.1) | collective-permute-done | bytes 1048608 | tf_op jit(solution)/shard_map/ppermute | solution.py:249
  121.5 6.9 %all-to-all-start.1 = ((f32[16,8,8,256]{3,2,1,0:T(8,128)}), f32[16,8,8,256]{3,2,1,0:T(8,128)S(1)}, u32[]{:S(2)}, u32[]{:S(2)}) async-start(f32[16,8,8,256]{3,2,1,0:T(8,128)} %add.46), calls=%async_computation.1 | async-start | bytes 2097152 | tf_op jit(solution)/shard_map/all_to_all | solution.py:253
  128.3 9.0 %forward.7 = (f32[16,8,8,256]{3,2,1,0:T(8,128)}, f32[16,8,8,256]{3,2,1,0:T(8,128)}) custom-call(s32[1]{0:T(128)} %bitcast.half_ref, s32[2]{0:T(128)} %kweights_ref.7, s32[2,2]{1,0:T(2,128)} %occ_ref.7, bf16[2,2,2,32,256,256]{5,4,3,2,1,0:T(8,128)(2,1)} %orb_ref.7, bf16[256,256]{1,0:T(8,128)(2,1)} %constant.41.clone.yh_ref, ...), custom_call_target="tpu_custom_call" | custom-call | flops 1610612736 | bytes 12582912 | tf_op jit(solution)/shard_map/forward/pallas_call | solution.py:88
  138.6 23.3 %collective-permute-done.3 = f32[16,8,8,256]{3,2,1,0:T(8,128)S(1)} collective-permute-done((f32[16,8,8,256]{3,2,1,0:T(8,128)}, f32[16,8,8,256]{3,2,1,0:T(8,128)S(1)}, u32[]{:S(2)}, u32[]{:S(2)}) %collective-permute-start.3) | collective-permute-done | bytes 1048608 | tf_op jit(solution)/shard_map/ppermute | solution.py:249
  164.2 6.9 %all-to-all-start.3 = ((f32[16,8,8,256]{3,2,1,0:T(8,128)}), f32[16,8,8,256]{3,2,1,0:T(8,128)S(1)}, u32[]{:S(2)}, u32[]{:S(2)}) async-start(f32[16,8,8,256]{3,2,1,0:T(8,128)} %add.48), calls=%async_computation.3 | async-start | bytes 2097152 | tf_op jit(solution)/shard_map/all_to_all | solution.py:253
  176.4 7.2 %project.3.refs_0_ = f32[8,512,256]{2,1,0:T(8,128)} custom-call(f32[16,8,8,256]{3,2,1,0:T(8,128)} %copy-done.5, bf16[4,512,128]{2,1,0:T(8,128)(2,1)} %get-tuple-element.27.th_ref, bf16[4,512,128]{2,1,0:T(8,128)(2,1)} %get-tuple-element.28.tl_ref), custom_call_target="tpu_custom_call" | custom-call | flops 805306368 | bytes 8388608 | tf_op jit(solution)/shard_map/project/pallas_call | solution.py:145
  183.6 8.1 %project.4.refs_0_ = f32[8,512,256]{2,1,0:T(8,128)} custom-call(f32[16,8,8,256]{3,2,1,0:T(8,128)} %copy-done.1, bf16[4,512,128]{2,1,0:T(8,128)(2,1)} %get-tuple-element.27.th_ref, bf16[4,512,128]{2,1,0:T(8,128)(2,1)} %get-tuple-element.28.tl_ref, f32[8,512,256]{2,1,0:T(8,128)} %project.3.refs_0_), custom_call_target="tpu_custom_call" | custom-call | flops 805306368 | bytes 8388608 | tf_op jit(solution)/shard_map/project/pallas_call | solution.py:145
  191.7 8.0 %project.5.part_ref = f32[8,512,256]{2,1,0:T(8,128)} custom-call(f32[16,8,8,256]{3,2,1,0:T(8,128)} %copy-done, bf16[4,512,128]{2,1,0:T(8,128)(2,1)} %get-tuple-element.27.th_ref, bf16[4,512,128]{2,1,0:T(8,128)(2,1)} %get-tuple-element.28.tl_ref, f32[8,512,256]{2,1,0:T(8,128)} %project.4.refs_0_), custom_call_target="tpu_custom_call" | custom-call | flops 805306368 | bytes 8388608 | tf_op jit(solution)/shard_map/project/pallas_call | solution.py:145
  200.7 9.4 %solve.1 = (f32[16,8,8,256]{3,2,1,0:T(8,128)}, bf16[8,512,256]{2,1,0:T(8,128)(2,1)}, bf16[8,512,256]{2,1,0:T(8,128)(2,1)}) custom-call(f32[8,512,256]{2,1,0:T(8,128)} %project.5.part_ref, f32[16,8,8,256]{3,2,1,0:T(8,128)} %copy-done.6, bf16[4,512,128]{2,1,0:T(8,128)(2,1)} %get-tuple-element.27.th_ref, bf16[4,512,128]{2,1,0:T(8,128)(2,1)} %get-tuple-element.28.tl_ref, ...), custom_call_target="tpu_custom_call" | custom-call | flops 1610612736 | bytes 12582912 | tf_op jit(solution)/shard_map/solve/pallas_call | solution.py:170
  210.1 6.0 %all-to-all-start.7 = ((f32[16,8,8,256]{3,2,1,0:T(8,128)}), f32[16,8,8,256]{3,2,1,0:T(8,128)S(1)}, u32[]{:S(2)}, u32[]{:S(2)}) async-start(f32[16,8,8,256]{3,2,1,0:T(8,128)} %get-tuple-element.40), calls=%async_computation.7 | async-start | bytes 2097152 | tf_op jit(solution)/shard_map/all_to_all | solution.py:253
  216.1 6.9 %filtered.5 = f32[16,8,8,256]{3,2,1,0:T(8,128)} custom-call(bf16[8,512,256]{2,1,0:T(8,128)(2,1)} %get-tuple-element.38.wh_ref, bf16[8,512,256]{2,1,0:T(8,128)(2,1)} %get-tuple-element.39.wl_ref, bf16[4,128,512]{2,1,0:T(8,128)(2,1)} %get-tuple-element.35.zh_ref, bf16[4,128,512]{2,1,0:T(8,128)(2,1)} %get-tuple-element.36.zl_ref), custom_call_target="tpu_custom_call" | custom-call | flops 805306368 | bytes 4194304 | tf_op jit(solution)/shard_map/filtered/pallas_call | solution.py:191
  223.0 18.0 %all-to-all-done.7.own_ref = f32[16,8,8,256]{3,2,1,0:T(8,128)S(1)} async-done(((f32[16,8,8,256]{3,2,1,0:T(8,128)}), f32[16,8,8,256]{3,2,1,0:T(8,128)S(1)}, u32[]{:S(2)}, u32[]{:S(2)}) %all-to-all-start.7) | async-done | bytes 1048608 | tf_op jit(solution)/shard_map/all_to_all | solution.py:253
  246.8 6.8 %filtered.4 = f32[16,8,8,256]{3,2,1,0:T(8,128)} custom-call(bf16[8,512,256]{2,1,0:T(8,128)(2,1)} %get-tuple-element.38.wh_ref, bf16[8,512,256]{2,1,0:T(8,128)(2,1)} %get-tuple-element.39.wl_ref, bf16[4,128,512]{2,1,0:T(8,128)(2,1)} %get-tuple-element.35.zh_ref, bf16[4,128,512]{2,1,0:T(8,128)(2,1)} %get-tuple-element.36.zl_ref), custom_call_target="tpu_custom_call" | custom-call | flops 805306368 | bytes 4194304 | tf_op jit(solution)/shard_map/filtered/pallas_call | solution.py:191
  253.6 18.0 %all-to-all-done.6.own_ref = f32[16,8,8,256]{3,2,1,0:T(8,128)S(1)} async-done(((f32[16,8,8,256]{3,2,1,0:T(8,128)}), f32[16,8,8,256]{3,2,1,0:T(8,128)S(1)}, u32[]{:S(2)}, u32[]{:S(2)}) %all-to-all-start.6) | async-done | bytes 1048608 | tf_op jit(solution)/shard_map/all_to_all | solution.py:253
  276.5 6.9 %filtered.3 = f32[16,8,8,256]{3,2,1,0:T(8,128)} custom-call(bf16[8,512,256]{2,1,0:T(8,128)(2,1)} %get-tuple-element.38.wh_ref, bf16[8,512,256]{2,1,0:T(8,128)(2,1)} %get-tuple-element.39.wl_ref, bf16[4,128,512]{2,1,0:T(8,128)(2,1)} %get-tuple-element.35.zh_ref, bf16[4,128,512]{2,1,0:T(8,128)(2,1)} %get-tuple-element.36.zl_ref), custom_call_target="tpu_custom_call" | custom-call | flops 805306368 | bytes 4194304 | tf_op jit(solution)/shard_map/filtered/pallas_call | solution.py:191
  283.3 18.0 %all-to-all-done.5.own_ref = f32[16,8,8,256]{3,2,1,0:T(8,128)S(1)} async-done(((f32[16,8,8,256]{3,2,1,0:T(8,128)}), f32[16,8,8,256]{3,2,1,0:T(8,128)S(1)}, u32[]{:S(2)}, u32[]{:S(2)}) %all-to-all-start.5) | async-done | bytes 1048608 | tf_op jit(solution)/shard_map/all_to_all | solution.py:253
  301.3 5.0 %all-to-all-start.4 = ((f32[16,8,8,256]{3,2,1,0:T(8,128)}), f32[16,8,8,256]{3,2,1,0:T(8,128)S(1)}, u32[]{:S(2)}, u32[]{:S(2)}) async-start(f32[16,8,8,256]{3,2,1,0:T(8,128)} %filtered.3), calls=%async_computation.4 | async-start | bytes 2097152 | tf_op jit(solution)/shard_map/all_to_all | solution.py:253
  309.0 22.6 %all-to-all-done.4.own_ref = f32[16,8,8,256]{3,2,1,0:T(8,128)S(1)} async-done(((f32[16,8,8,256]{3,2,1,0:T(8,128)}), f32[16,8,8,256]{3,2,1,0:T(8,128)S(1)}, u32[]{:S(2)}, u32[]{:S(2)}) %all-to-all-start.4) | async-done | bytes 1048608 | tf_op jit(solution)/shard_map/all_to_all | solution.py:253
  332.8 6.7 %inverse.4.refs_0_ = f32[32,256,256]{2,1,0:T(8,128)} custom-call(s32[1]{0:T(128)} %bitcast.half_ref, f32[16,8,8,256]{3,2,1,0:T(8,128)} %copy-done.7, f32[16,8,8,256]{3,2,1,0:T(8,128)} %collective-permute-done.7.other_ref, bf16[256,256]{1,0:T(8,128)(2,1)} %constant.45.clone.yh_ref, bf16[256,256]{1,0:T(8,128)(2,1)} %constant.46.clone.yl_ref, ...), custom_call_target="tpu_custom_call" | custom-call | flops 1610612736 | bytes 4194304 | tf_op jit(solution)/shard_map/inverse/pallas_call | solution.py:225
  339.5 13.9 %collective-permute-done.6.other_ref = f32[16,8,8,256]{3,2,1,0:T(8,128)} collective-permute-done((f32[16,8,8,256]{3,2,1,0:T(8,128)S(1)}, f32[16,8,8,256]{3,2,1,0:T(8,128)}, u32[]{:S(2)}, u32[]{:S(2)}) %collective-permute-start.6) | collective-permute-done | bytes 1048608 | tf_op jit(solution)/shard_map/ppermute | solution.py:249
  353.4 6.7 %inverse.5.refs_0_ = f32[32,256,256]{2,1,0:T(8,128)} custom-call(s32[1]{0:T(128)} %bitcast.half_ref, f32[16,8,8,256]{3,2,1,0:T(8,128)} %copy-done.2, f32[16,8,8,256]{3,2,1,0:T(8,128)} %collective-permute-done.6.other_ref, bf16[256,256]{1,0:T(8,128)(2,1)} %constant.45.clone.yh_ref, ...), custom_call_target="tpu_custom_call", output_to_operand_aliasing={{}: (7, {})} | custom-call | flops 1610612736 | bytes 4194304 | tf_op jit(solution)/shard_map/inverse/pallas_call | solution.py:225
  360.2 15.8 %collective-permute-done.5.other_ref = f32[16,8,8,256]{3,2,1,0:T(8,128)} collective-permute-done((f32[16,8,8,256]{3,2,1,0:T(8,128)S(1)}, f32[16,8,8,256]{3,2,1,0:T(8,128)}, u32[]{:S(2)}, u32[]{:S(2)}) %collective-permute-start.5) | collective-permute-done | bytes 1048608 | tf_op jit(solution)/shard_map/ppermute | solution.py:249
  375.9 6.7 %inverse.6.refs_0_ = f32[32,256,256]{2,1,0:T(8,128)} custom-call(s32[1]{0:T(128)} %bitcast.half_ref, f32[16,8,8,256]{3,2,1,0:T(8,128)} %copy-done.3, f32[16,8,8,256]{3,2,1,0:T(8,128)} %collective-permute-done.5.other_ref, bf16[256,256]{1,0:T(8,128)(2,1)} %constant.45.clone.yh_ref, ...), custom_call_target="tpu_custom_call", output_to_operand_aliasing={{}: (7, {})} | custom-call | flops 1610612736 | bytes 4194304 | tf_op jit(solution)/shard_map/inverse/pallas_call | solution.py:225
  382.6 15.8 %collective-permute-done.4.other_ref = f32[16,8,8,256]{3,2,1,0:T(8,128)} collective-permute-done((f32[16,8,8,256]{3,2,1,0:T(8,128)S(1)}, f32[16,8,8,256]{3,2,1,0:T(8,128)}, u32[]{:S(2)}, u32[]{:S(2)}) %collective-permute-start.4) | collective-permute-done | bytes 1048608 | tf_op jit(solution)/shard_map/ppermute | solution.py:249
  398.4 6.7 %inverse.7 = f32[32,256,256]{2,1,0:T(8,128)} custom-call(s32[1]{0:T(128)} %bitcast.half_ref, f32[16,8,8,256]{3,2,1,0:T(8,128)} %copy-done.4, f32[16,8,8,256]{3,2,1,0:T(8,128)} %collective-permute-done.4.other_ref, bf16[256,256]{1,0:T(8,128)(2,1)} %constant.45.clone.yh_ref, bf16[256,256]{1,0:T(8,128)(2,1)} %constant.46.clone.yl_ref, ...), custom_call_target="tpu_custom_call", output_to_operand_aliasing={{}: (7, {})} | custom-call | flops 1610612736 | bytes 4194304 | tf_op jit(solution)/shard_map/inverse/pallas_call | solution.py:225
  (42 shorter events, 35.1 us)
Async XLA Ops:
  8.9 24.2 %collective-permute-start.2 = (f32[16,8,8,256]{3,2,1,0:T(8,128)}, f32[16,8,8,256]{3,2,1,0:T(8,128)S(1)}, u32[]{:S(2)}, u32[]{:S(2)}) collective-permute-start(f32[16,8,8,256]{3,2,1,0:T(8,128)} %get-tuple-element.32), channel_id=1, source_target_pairs={{0,16},{16,0},{1,17},{17,1},{2,18},{18,2},{3,19},{19,3},{4,20},{20... | collective-permute-start | bytes 3145736 | tf_op jit(solution)/shard_map/ppermute | solution.py:249
  35.5 43.2 %all-to-all-start.2 = ((f32[16,8,8,256]{3,2,1,0:T(8,128)}), f32[16,8,8,256]{3,2,1,0:T(8,128)S(1)}, u32[]{:S(2)}, u32[]{:S(2)}) async-start(f32[16,8,8,256]{3,2,1,0:T(8,128)} %add.47), calls=%async_computation.2 | async-start | bytes 2097152 | tf_op jit(solution)/shard_map/all_to_all | solution.py:253
  51.9 24.5 %collective-permute-start = (f32[16,8,8,256]{3,2,1,0:T(8,128)}, f32[16,8,8,256]{3,2,1,0:T(8,128)S(1)}, u32[]{:S(2)}, u32[]{:S(2)}) collective-permute-start(f32[16,8,8,256]{3,2,1,0:T(8,128)} %get-tuple-element.24), channel_id=1, source_target_pairs={{0,16},{16,0},{1,17},{17,1},{2,18},{18,2},{3,19},{19,3},{4,20},{20... | collective-permute-start | bytes 3145736 | tf_op jit(solution)/shard_map/ppermute | solution.py:249
  78.7 15.8 %copy-start.5 = (f32[16,8,8,256]{3,2,1,0:T(8,128)}, f32[16,8,8,256]{3,2,1,0:T(8,128)S(1)}, u32[]{:S(2)}) copy-start(f32[16,8,8,256]{3,2,1,0:T(8,128)S(1)} %all-to-all-done.2.x_ref) | copy-start | bytes 3145732
  78.8 42.7 %all-to-all-start = ((f32[16,8,8,256]{3,2,1,0:T(8,128)}), f32[16,8,8,256]{3,2,1,0:T(8,128)S(1)}, u32[]{:S(2)}, u32[]{:S(2)}) async-start(f32[16,8,8,256]{3,2,1,0:T(8,128)} %add.45), calls=%async_computation | async-start | bytes 2097152 | tf_op jit(solution)/shard_map/all_to_all | solution.py:253
  94.6 24.5 %collective-permute-start.1 = (f32[16,8,8,256]{3,2,1,0:T(8,128)}, f32[16,8,8,256]{3,2,1,0:T(8,128)S(1)}, u32[]{:S(2)}, u32[]{:S(2)}) collective-permute-start(f32[16,8,8,256]{3,2,1,0:T(8,128)} %get-tuple-element.30), channel_id=1, source_target_pairs={{0,16},{16,0},{1,17},{17,1},{2,18},{18,2},{3,19},{19,3},{4,20},{20... | collective-permute-start | bytes 3145736 | tf_op jit(solution)/shard_map/ppermute | solution.py:249
  121.5 15.9 %copy-start = (f32[16,8,8,256]{3,2,1,0:T(8,128)}, f32[16,8,8,256]{3,2,1,0:T(8,128)S(1)}, u32[]{:S(2)}) copy-start(f32[16,8,8,256]{3,2,1,0:T(8,128)S(1)} %all-to-all-done.x_ref) | copy-start | bytes 3145732
  121.5 42.8 %all-to-all-start.1 = ((f32[16,8,8,256]{3,2,1,0:T(8,128)}), f32[16,8,8,256]{3,2,1,0:T(8,128)S(1)}, u32[]{:S(2)}, u32[]{:S(2)}) async-start(f32[16,8,8,256]{3,2,1,0:T(8,128)} %add.46), calls=%async_computation.1 | async-start | bytes 2097152 | tf_op jit(solution)/shard_map/all_to_all | solution.py:253
  128.3 42.8 %copy-start.8 = (f32[512]{0:T(512)S(1)}, f32[512]{0:T(512)}, u32[]{:S(2)}) copy-start(f32[512]{0:T(512)} %param.17) | copy-start | bytes 6148
  137.3 24.5 %collective-permute-start.3 = (f32[16,8,8,256]{3,2,1,0:T(8,128)}, f32[16,8,8,256]{3,2,1,0:T(8,128)S(1)}, u32[]{:S(2)}, u32[]{:S(2)}) collective-permute-start(f32[16,8,8,256]{3,2,1,0:T(8,128)} %get-tuple-element.34), channel_id=1, source_target_pairs={{0,16},{16,0},{1,17},{17,1},{2,18},{18,2},{3,19},{19,3},{4,20},{20... | collective-permute-start | bytes 3145736 | tf_op jit(solution)/shard_map/ppermute | solution.py:249
  164.2 19.4 %copy-start.1 = (f32[16,8,8,256]{3,2,1,0:T(8,128)}, f32[16,8,8,256]{3,2,1,0:T(8,128)S(1)}, u32[]{:S(2)}) copy-start(f32[16,8,8,256]{3,2,1,0:T(8,128)S(1)} %all-to-all-done.1.x_ref) | copy-start | bytes 3145732
  164.2 35.5 %all-to-all-start.3 = ((f32[16,8,8,256]{3,2,1,0:T(8,128)}), f32[16,8,8,256]{3,2,1,0:T(8,128)S(1)}, u32[]{:S(2)}, u32[]{:S(2)}) async-start(f32[16,8,8,256]{3,2,1,0:T(8,128)} %add.48), calls=%async_computation.3 | async-start | bytes 2097152 | tf_op jit(solution)/shard_map/all_to_all | solution.py:253
  199.7 1.0 copy-start.6
  210.1 30.9 %all-to-all-start.7 = ((f32[16,8,8,256]{3,2,1,0:T(8,128)}), f32[16,8,8,256]{3,2,1,0:T(8,128)S(1)}, u32[]{:S(2)}, u32[]{:S(2)}) async-start(f32[16,8,8,256]{3,2,1,0:T(8,128)} %get-tuple-element.40), calls=%async_computation.7 | async-start | bytes 2097152 | tf_op jit(solution)/shard_map/all_to_all | solution.py:253
  241.0 1.0 copy-start.7
  242.0 29.7 %all-to-all-start.6 = ((f32[16,8,8,256]{3,2,1,0:T(8,128)}), f32[16,8,8,256]{3,2,1,0:T(8,128)S(1)}, u32[]{:S(2)}, u32[]{:S(2)}) async-start(f32[16,8,8,256]{3,2,1,0:T(8,128)} %filtered.5), calls=%async_computation.6 | async-start | bytes 2097152 | tf_op jit(solution)/shard_map/all_to_all | solution.py:253
  271.6 67.9 %copy-start.2 = (f32[16,8,8,256]{3,2,1,0:T(8,128)}, f32[16,8,8,256]{3,2,1,0:T(8,128)S(1)}, u32[]{:S(2)}) copy-start(f32[16,8,8,256]{3,2,1,0:T(8,128)S(1)} %all-to-all-done.6.own_ref) | copy-start | bytes 3145732
  271.6 29.7 %all-to-all-start.5 = ((f32[16,8,8,256]{3,2,1,0:T(8,128)}), f32[16,8,8,256]{3,2,1,0:T(8,128)S(1)}, u32[]{:S(2)}, u32[]{:S(2)}) async-start(f32[16,8,8,256]{3,2,1,0:T(8,128)} %filtered.4), calls=%async_computation.5 | async-start | bytes 2097152 | tf_op jit(solution)/shard_map/all_to_all | solution.py:253
  301.3 58.8 %copy-start.3 = (f32[16,8,8,256]{3,2,1,0:T(8,128)}, f32[16,8,8,256]{3,2,1,0:T(8,128)S(1)}, u32[]{:S(2)}) copy-start(f32[16,8,8,256]{3,2,1,0:T(8,128)S(1)} %all-to-all-done.5.own_ref) | copy-start | bytes 3145732
  301.3 30.3 %all-to-all-start.4 = ((f32[16,8,8,256]{3,2,1,0:T(8,128)}), f32[16,8,8,256]{3,2,1,0:T(8,128)S(1)}, u32[]{:S(2)}, u32[]{:S(2)}) async-start(f32[16,8,8,256]{3,2,1,0:T(8,128)} %filtered.3), calls=%async_computation.4 | async-start | bytes 2097152 | tf_op jit(solution)/shard_map/all_to_all | solution.py:253
  306.3 26.5 %collective-permute-start.7 = (f32[16,8,8,256]{3,2,1,0:T(8,128)}, f32[16,8,8,256]{3,2,1,0:T(8,128)}, u32[]{:S(2)}, u32[]{:S(2)}) collective-permute-start(f32[16,8,8,256]{3,2,1,0:T(8,128)} %copy-done.7), channel_id=1, source_target_pairs={{0,16},{16,0},{1,17},{17,1},{2,18},{18,2},{3,19},{19,3},{4,20},{20... | collective-permute-start | bytes 3145736 | tf_op jit(solution)/shard_map/ppermute | solution.py:249
  307.5 45.9 %collective-permute-start.6 = (f32[16,8,8,256]{3,2,1,0:T(8,128)S(1)}, f32[16,8,8,256]{3,2,1,0:T(8,128)}, u32[]{:S(2)}, u32[]{:S(2)}) collective-permute-start(f32[16,8,8,256]{3,2,1,0:T(8,128)S(1)} %all-to-all-done.6.own_ref), channel_id=1, source_target_pairs={{0,16},{16,0},{1,17},{17,1},{2,18},{18,2},{3,19},{19,3},{4,20},{20... | collective-permute-start | bytes 3145736 | tf_op jit(solution)/shard_map/ppermute | solution.py:249
  307.8 68.1 %collective-permute-start.5 = (f32[16,8,8,256]{3,2,1,0:T(8,128)S(1)}, f32[16,8,8,256]{3,2,1,0:T(8,128)}, u32[]{:S(2)}, u32[]{:S(2)}) collective-permute-start(f32[16,8,8,256]{3,2,1,0:T(8,128)S(1)} %all-to-all-done.5.own_ref), channel_id=1, source_target_pairs={{0,16},{16,0},{1,17},{17,1},{2,18},{18,2},{3,19},{19,3},{4,20},{20... | collective-permute-start | bytes 3145736 | tf_op jit(solution)/shard_map/ppermute | solution.py:249
  331.6 28.6 %copy-start.4 = (f32[16,8,8,256]{3,2,1,0:T(8,128)}, f32[16,8,8,256]{3,2,1,0:T(8,128)S(1)}, u32[]{:S(2)}) copy-start(f32[16,8,8,256]{3,2,1,0:T(8,128)S(1)} %all-to-all-done.4.own_ref) | copy-start | bytes 3145732
  331.6 66.8 %collective-permute-start.4 = (f32[16,8,8,256]{3,2,1,0:T(8,128)S(1)}, f32[16,8,8,256]{3,2,1,0:T(8,128)}, u32[]{:S(2)}, u32[]{:S(2)}) collective-permute-start(f32[16,8,8,256]{3,2,1,0:T(8,128)S(1)} %all-to-all-done.4.own_ref), channel_id=1, source_target_pairs={{0,16},{16,0},{1,17},{17,1},{2,18},{18,2},{3,19},{19,3},{4,20},{20... | collective-permute-start | bytes 3145736 | tf_op jit(solution)/shard_map/ppermute | solution.py:249

commit v2 on v1

--- a/solution.py
+++ b/solution.py
@@ -52,16 +52,17 @@
 
 
 GROUP = 8
-
-
-def forward(orbitals, kweights, occupations, half, tables, chunk, blocks, step=2):
+INNER = 4
+
+
+def forward(orbitals, kweights, occupations, half, tables, chunk, blocks, plain, step=2):
     points, bands, parts, _, nx, ny = orbitals.shape
     rows = nx // (2 * blocks)
     steps = GROUP // step
     scale = 1.0 / (16.0 * points * bands)
 
     def body(half_ref, kweights_ref, occ_ref, orb_ref, yh_ref, yl_ref, xh_ref, xl_ref, own_ref, other_ref, s_ref):
-        mine = half_ref[0]
+        mine, place = half_ref[0], half_ref[1]
         here = pl.program_id(0)
         yh, yl = yh_ref[...], yl_ref[...]
         for plane in range(step):
@@ -80,9 +81,10 @@
         @pl.when(here == steps - 1)
         def _():
             for slot, out in ((0, own_ref), (1, other_ref)):
-                first = pl.multiple_of((mine if slot == 0 else 1 - mine) * (nx // 2), nx // 2)
-                for plane in range(GROUP):
-                    out[:, :, plane, :] = s_ref[plane, pl.ds(first, nx // 2), :].reshape(blocks, rows, ny)
+                for block in range(blocks):
+                    first = ((mine if slot == 0 else 1 - mine) * blocks + (block if plain else place ^ block)) * rows
+                    for plane in range(GROUP):
+                        out[block, :, plane, :] = s_ref[plane, pl.ds(pl.multiple_of(first, rows), rows), :]
 
     out_shape = jax.ShapeDtypeStruct((blocks, rows, GROUP, ny), f32)
     return pl.pallas_call(
@@ -99,31 +101,49 @@
     )(half, kweights, occupations, orbitals, *tables)
 
 
-def prepare(z_basis, blocks, planes):
+def prepare(z_basis, half, blocks, planes):
     nz = z_basis.shape[0]
     chunks = planes // GROUP
     size = blocks * GROUP
 
-    def body(z_ref, zh_ref, zl_ref, th_ref, tl_ref):
-        value = z_ref[...].reshape(size, nz)
-        zh_ref[0], zl_ref[0] = split(value)
-        th_ref[0], tl_ref[0] = split(value.T)
+    def body(half_ref, z_ref, zh_ref, zl_ref, th_ref, tl_ref):
+        order = [outer * INNER + inner for inner in range(INNER) for outer in range(blocks // INNER)]
+        here = pl.program_id(0)
+
+        def rows_of(plain):
+            places = [jnp.where(plain, n, half_ref[1] ^ block) for n, block in enumerate(order)]
+            return jnp.concatenate([z_ref[place] for place in places], axis=0)
+
+        zh_ref[0], zl_ref[0] = split(rows_of(here == 0))
+        th_ref[0], tl_ref[0] = split(rows_of(here == chunks - 1).T)
 
     straight = jax.ShapeDtypeStruct((chunks, size, nz), bf16)
     turned = jax.ShapeDtypeStruct((chunks, nz, size), bf16)
     return pl.pallas_call(
         body,
         grid=(chunks,),
-        in_specs=[pl.BlockSpec((blocks, GROUP, nz), lambda i: (0, i, 0))],
+        in_specs=[smem(), pl.BlockSpec((blocks, GROUP, nz), lambda i: (0, i, 0))],
         out_specs=[pl.BlockSpec((1, size, nz), lambda i: (i, 0, 0))] * 2 + [pl.BlockSpec((1, nz, size), lambda i: (i, 0, 0))] * 2,
         out_shape=[straight] * 2 + [turned] * 2,
         cost_estimate=cost(nz * nz * 100, nz * nz * 12),
         name="prepare",
-    )(z_basis.reshape(blocks, planes, nz))
-
-
-def by_row(blocks, ny):
-    return pl.BlockSpec((blocks, 1, GROUP, ny), lambda i: (0, i, 0, 0))
+    )(half, z_basis.reshape(blocks, planes, nz))
+
+
+def by_row(part):
+    return pl.BlockSpec((part.shape[0], 1) + part.shape[2:], lambda i: (0, i, 0, 0))
+
+
+def gather_row(refs, ny):
+    return jnp.concatenate([ref[:, 0].reshape(-1, ny) for ref in refs], axis=0)
+
+
+def scatter_row(refs, value):
+    first = 0
+    for ref in refs:
+        size = ref.shape[0] * GROUP
+        ref[:, 0] = value[first : first + size].reshape(ref.shape[0], GROUP, value.shape[1])
+        first += size
 
 
 def one_chunk(table, chunk):
@@ -131,102 +151,113 @@
 
 
 def project(columns, turned, chunk, before):
-    blocks, rows, _, ny = columns.shape
-    nz = turned[0].shape[1]
-    size = blocks * GROUP
+    rows, _, ny = columns[0].shape[1:]
+    nz, size = turned[0].shape[1:]
+    many = len(columns)
     extra = () if before is None else (before,)
 
-    def body(x_ref, th_ref, tl_ref, *refs):
-        xh, xl = split(x_ref[:, 0].reshape(size, ny))
-        value = dot3(th_ref[0], tl_ref[0], xh, xl)
-        refs[-1][0] = value if before is None else value + refs[0][0]
+    def body(*refs):
+        xh, xl = split(gather_row(refs[:many], ny))
+        value = dot3(refs[many][0], refs[many + 1][0], xh, xl)
+        refs[-1][0] = value if before is None else value + refs[many + 2][0]
 
     part = pl.BlockSpec((1, nz, ny), lambda i: (i, 0, 0))
     return pl.pallas_call(
         body,
         grid=(rows,),
-        in_specs=[by_row(blocks, ny)] + [one_chunk(t, chunk) for t in turned] + [part for _ in extra],
+        in_specs=[by_row(c) for c in columns] + [one_chunk(t, chunk) for t in turned] + [part for _ in extra],
         out_specs=part,
         out_shape=jax.ShapeDtypeStruct((rows, nz, ny), f32),
         cost_estimate=cost(6 * nz * size * rows * ny, 8 * nz * rows * ny),
         name="project",
-    )(columns, *turned, *extra)
+    )(*columns, *turned, *extra)
 
 
 def solve(part, columns, straight, turned, eigen, shift, chunk):
-    blocks, rows, _, ny = columns.shape
-    nz = turned[0].shape[1]
-    size = blocks * GROUP
-
-    def body(part_ref, x_ref, th_ref, tl_ref, zh_ref, zl_ref, e_ref, s_ref, out_ref, wh_ref, wl_ref):
-        xh, xl = split(x_ref[:, 0].reshape(size, ny))
+    rows, _, ny = columns[0].shape[1:]
+    nz, size = turned[0].shape[1:]
+    many = len(columns)
+
+    def body(part_ref, *refs):
+        th_ref, tl_ref, zh_ref, zl_ref, e_ref, s_ref = refs[many : many + 6]
+        wh_ref, wl_ref = refs[-2:]
+        xh, xl = split(gather_row(refs[:many], ny))
         projected = part_ref[0] + dot3(th_ref[0], tl_ref[0], xh, xl)
         wh, wl = split(projected / (e_ref[...] + s_ref[0]))
         wh_ref[0], wl_ref[0] = wh, wl
-        out_ref[:, 0] = dot3(zh_ref[0], zl_ref[0], wh, wl).reshape(blocks, GROUP, ny)
+        scatter_row(refs[many + 6 : -2], dot3(zh_ref[0], zl_ref[0], wh, wl))
 
     w_spec = pl.BlockSpec((1, nz, ny), lambda i: (i, 0, 0))
     w_shape = jax.ShapeDtypeStruct((rows, nz, ny), bf16)
-    return pl.pallas_call(
+    *ready, wh, wl = pl.pallas_call(
         body,
         grid=(rows,),
-        in_specs=[w_spec, by_row(blocks, ny)]
+        in_specs=[w_spec]
+        + [by_row(c) for c in columns]
         + [one_chunk(t, chunk) for t in turned]
         + [one_chunk(z, 0) for z in straight]
         + [whole(eigen.shape), pl.BlockSpec((1, 1, ny), lambda i: (i, 0, 0))],
-        out_specs=[by_row(blocks, ny), w_spec, w_spec],
-        out_shape=[jax.ShapeDtypeStruct(columns.shape, f32), w_shape, w_shape],
+        out_specs=[by_row(c) for c in columns] + [w_spec, w_spec],
+        out_shape=[jax.ShapeDtypeStruct(c.shape, f32) for c in columns] + [w_shape, w_shape],
         cost_estimate=cost(12 * nz * rows * ny * size, 12 * nz * rows * ny),
         name="solve",
-    )(part, columns, *turned, *straight, eigen, shift)
-
-
-def filtered(wh, wl, straight, chunk, blocks):
+    )(part, *columns, *turned, *straight, eigen, shift)
+    return ready, wh, wl
+
+
+def filtered(wh, wl, straight, chunk, like):
     rows, nz, ny = wh.shape
 
-    def body(wh_ref, wl_ref, zh_ref, zl_ref, out_ref):
-        out_ref[:, 0] = dot3(zh_ref[0], zl_ref[0], wh_ref[0], wl_ref[0]).reshape(blocks, GROUP, ny)
+    def body(wh_ref, wl_ref, zh_ref, zl_ref, *refs):
+        scatter_row(refs, dot3(zh_ref[0], zl_ref[0], wh_ref[0], wl_ref[0]))
 
     w_spec = pl.BlockSpec((1, nz, ny), lambda i: (i, 0, 0))
     return pl.pallas_call(
         body,
         grid=(rows,),
         in_specs=[w_spec, w_spec] + [one_chunk(z, chunk) for z in straight],
-        out_specs=by_row(blocks, ny),
-        out_shape=jax.ShapeDtypeStruct((blocks, rows, GROUP, ny), f32),
-        cost_estimate=cost(6 * nz * rows * ny * blocks * GROUP, 4 * nz * rows * ny),
+        out_specs=[by_row(c) for c in like],
+        out_shape=[jax.ShapeDtypeStruct(c.shape, f32) for c in like],
+        cost_estimate=cost(6 * nz * rows * ny * straight[0].shape[1], 4 * nz * rows * ny),
         name="filtered",
     )(wh, wl, *straight)
 
 
-def inverse(own, other, half, tables, planes, chunk, into, step=2):
-    blocks, rows, _, ny = own.shape
+def inverse(own, other, half, tables, planes, chunk, into, plain, step=2):
+    lead, rows, _, ny = own[0].shape
+    blocks = len(own) * lead
     nx = 2 * blocks * rows
     steps = GROUP // step
     extra = () if into is None else (into,)
 
-    def body(half_ref, own_ref, other_ref, yh_ref, yl_ref, xh_ref, xl_ref, *refs):
+    def body(half_ref, *refs):
         out_ref, f_ref = refs[-2:]
+        yh_ref, yl_ref, xh_ref, xl_ref = refs[2 * len(own) : 2 * len(own) + 4]
         here = pl.program_id(0)
 
         @pl.when(here == 0)
         def _():
-            for slot, ref in ((0, own_ref), (1, other_ref)):
-                first = pl.multiple_of((half_ref[0] if slot == 0 else 1 - half_ref[0]) * (nx // 2), nx // 2)
-                for plane in range(GROUP):
-                    f_ref[plane, pl.ds(first, nx // 2), :] = ref[:, :, plane, :].reshape(nx // 2, ny)
+            for slot in range(2):
+                for outer in range(len(own)):
+                    for inner in range(lead):
+                        block = outer * lead + inner
+                        block = block if plain else half_ref[1] ^ block
+                        first = ((half_ref[0] if slot == 0 else 1 - half_ref[0]) * blocks + block) * rows
+                        for plane in range(GROUP):
+                            value = refs[slot * len(own) + outer][inner, :, plane, :]
+                            f_ref[plane, pl.ds(pl.multiple_of(first, rows), rows), :] = value
 
         for plane in range(step):
             fh, fl = split(f_ref[here * step + plane])
             hh, hl = split(dot3(fh, fl, yh_ref[...], yl_ref[...]))
             out_ref[plane] = dot3(xh_ref[...], xl_ref[...], hh, hl)
 
-    operands = (half, own, other, *tables, *extra)
+    operands = (half, *own, *other, *tables, *extra)
     return pl.pallas_call(
         body,
         grid=(steps,),
-        in_specs=[smem(), whole(own.shape), whole(other.shape)]
-        + [whole(t.shape) for t in tables]
+        in_specs=[smem()]
+        + [whole(v.shape) for v in (*own, *other, *tables)]
         + [pl.BlockSpec(memory_space=pl.ANY) for _ in extra],
         out_specs=pl.BlockSpec((step, nx, ny), lambda i: (chunk * steps + i, 0, 0)),
         out_shape=jax.ShapeDtypeStruct((planes, nx, ny), f32),
@@ -249,6 +280,38 @@
     return lax.ppermute(value, "kpt", [(0, 1), (1, 0)])
 
 
+def pairwise(value, distance):
+    count = lax.axis_size("grid")
+    return lax.ppermute(value, "grid", [(place, place ^ distance) for place in range(count)])
+
+
+def across(parts, unit):
+    return [parts[0]] + [pairwise(parts[n], n * unit) for n in range(1, len(parts))]
+
+
+def turn(parts):
+    _, rows, _, ny = parts[0].shape
+    many = len(parts)
+
+    def body(*refs):
+        for b in range(parts[0].shape[0]):
+            for a in range(many):
+                refs[many + b][a] = refs[a][b]
+
+    spec = [pl.BlockSpec((n, rows // 2, GROUP, ny), lambda i: (0, i, 0, 0)) for n in (parts[0].shape[0], many)]
+    shape = jax.ShapeDtypeStruct((many, rows, GROUP, ny), f32)
+    size = rows * GROUP * ny * many * parts[0].shape[0]
+    return pl.pallas_call(
+        body,
+        grid=(2,),
+        in_specs=[spec[0]] * many,
+        out_specs=[spec[1]] * parts[0].shape[0],
+        out_shape=[shape] * parts[0].shape[0],
+        cost_estimate=cost(size * 100, size * 8),
+        name="turn",
+    )(*parts)
+
+
 def exchange(value):
     return lax.all_to_all(value, "grid", split_axis=0, concat_axis=0, tiled=True)
 
@@ -259,7 +322,7 @@
     rows = nx // (2 * blocks)
     chunks = planes // GROUP
     mine = lax.axis_index("kpt").astype(jnp.int32)
-    half = mine.reshape(1)
+    half = jnp.stack([mine, lax.axis_index("grid").astype(jnp.int32)])
     table_x, scaled_x = real_basis(nx)
     table_y, scaled_y = real_basis(ny)
     to_modes = (*split_const(np.ascontiguousarray(table_y.T)), *split_const(table_x))
@@ -267,13 +330,20 @@
 
     columns = []
     for chunk in range(chunks):
-        own, other = forward(orbitals, kweights, occupations, half, to_modes, chunk, blocks)
+        last = chunk == chunks - 1
+        own, other = forward(orbitals, kweights, occupations, half, to_modes, chunk, blocks, last)
         if chunk == 0:
             z_basis, z_eigen, own = lax.optimization_barrier((z_basis, z_eigen, own))
         other = swap(other)
-        own = own + other
-        columns.append(exchange(own))
-    zh, zl, th, tl = prepare(z_basis, blocks, planes)
+        if last:
+            own = own + other
+            columns.append([exchange(own)])
+            break
+        parts = [own[n : n + INNER] + other[n : n + INNER] for n in range(0, blocks, INNER)]
+        parts = across(parts, INNER)
+        parts = turn(parts)
+        columns.append(across(parts, 1))
+    zh, zl, th, tl = prepare(z_basis, half, blocks, planes)
     first = (mine * blocks + lax.axis_index("grid")) * rows
     shift = row_shift(first, rows, nx, ny)[:, None, :]
     part = None
@@ -284,10 +354,15 @@
     ready, wh, wl = solve(part, columns[-1], (zh, zl), (th, tl), z_eigen[:, None], shift, chunks - 1)
     out = None
     for chunk in range(chunks):
-        ready = ready if chunk == 0 else filtered(wh, wl, (zh, zl), chunk, blocks)
-        own = exchange(ready)
-        other = swap(own)
-        out = inverse(own, other, half, to_grid, planes, chunk, out)
+        if chunk == 0:
+            own = [exchange(ready[0])]
+        else:
+            ready = filtered(wh, wl, (zh, zl), chunk, columns[0])
+            parts = across(ready, 1)
+            parts = turn(parts)
+            own = across(parts, INNER)
+        other = [swap(v) for v in own]
+        out = inverse(own, other, half, to_grid, planes, chunk, out, chunk == 0)
     return out
 
 
@@ -322,7 +397,8 @@
 def whole_tiles(shape, blocks):
     planes, nx, ny = shape[3:]
     rows = nx // (2 * blocks)
-    return rows % 8 == 0 and ny % 128 == 0 and nx % 256 == 0 and planes % GROUP == 0
+    paired = blocks % INNER == 0 and blocks & (blocks - 1) == 0
+    return paired and rows % 8 == 0 and ny % 128 == 0 and nx % 256 == 0 and planes % GROUP == 0
 
 
 def on_device(orbitals, *rest):

time: 410 us -> 369 us (0.900)
  waiting for transfers between devices: 215 us -> 149 us
  Pallas kernels: 120 us -> 133 us
  starting transfers between devices: 57.4 us -> 64.2 us
  local copies, waits for them, and re-layouts: 2.89 us -> 8.07 us
    ppermute x0 -> x36, waiting for transfers between devices: none -> 92 us  [pairwise(): lax.ppermute(value, 'grid', [(place, place ^ distance) for place in range...]
    ppermute x8 -> x17, waiting for transfers between devices: 138 us -> 57.4 us  [swap(): return lax.ppermute(value, 'kpt', [(0, 1), (1, 0)])]
    all_to_all x8 -> x2, waiting for transfers between devices: 76.6 us -> 0.01 us  [exchange(): lax.all_to_all(value, 'grid', split_axis=0, concat_axis=0, tiled=True)]
    all_to_all x8 -> x2, starting transfers between devices: 48.7 us -> 14.2 us  [exchange(): lax.all_to_all(value, 'grid', split_axis=0, concat_axis=0, tiled=True)]
    ppermute x0 -> x36, starting transfers between devices: none -> 34.1 us  [pairwise(): lax.ppermute(value, 'grid', [(place, place ^ distance) for place in range...]
    pallas_call x9 -> x15, Pallas kernels: 63.1 us -> 76.5 us  [the longest x4 27.1 us: inverse(): pl.pallas_call(body, grid=(steps,), in_specs=[smem()] + [whole(v.shape) f...]
    ppermute x8 -> x17, starting transfers between devices: 8.72 us -> 15.9 us  [swap(): return lax.ppermute(value, 'kpt', [(0, 1), (1, 0)])]
    add x4 -> x1, other arithmetic: 9.35 us -> 2.36 us  [on_device_kernels(): own = own + other]
  transfers between devices with their start and end apart: 16 -> 55, of which waited for: 11 -> 23; matrix products, arithmetic and copies ran while one was open for 2% -> 3% of each run, Pallas kernels for 23% -> 30%
where the time goes in v2:
time: 369 us; the launch traced here: 364 us
  waiting for transfers between devices  149 us (40%)
  Pallas kernels  133 us (36%)
  starting transfers between devices  64.2 us (17%)
  other arithmetic  9.55 us (3%)
  local copies, waits for them, and re-layouts  8.07 us (2%)
    ppermute x36, waiting for transfers between devices, pairwise(): lax.ppermute(value, 'grid', [(place, place ^ distance) for place in range...  92 us
    ppermute x17, waiting for transfers between devices, swap(): return lax.ppermute(value, 'kpt', [(0, 1), (1, 0)])  57.4 us
    pallas_call x4, Pallas kernels, forward(): pl.pallas_call(body, grid=(steps,), in_specs=[smem(), smem(), smem()] + [...  35.8 us
    ppermute x36, starting transfers between devices, pairwise(): lax.ppermute(value, 'grid', [(place, place ^ distance) for place in range...  34.1 us
    pallas_call x4, Pallas kernels, inverse(): pl.pallas_call(body, grid=(steps,), in_specs=[smem()] + [whole(v.shape) f...  27.1 us
    pallas_call x3, Pallas kernels, project(): pl.pallas_call(body, grid=(rows,), in_specs=[by_row(c) for c in columns]...  23.2 us
    pallas_call x3, Pallas kernels, filtered(): pl.pallas_call(body, grid=(rows,), in_specs=[w_spec, w_spec] + [one_chunk...  20.3 us
    ppermute x17, starting transfers between devices, swap(): return lax.ppermute(value, 'kpt', [(0, 1), (1, 0)])  15.9 us
  transfers between devices with their start and end apart: 55, of which 23 were waited for; matrix products, arithmetic and copies ran while one was open for 3% of the time, Pallas kernels for 30%

profile of v2, /device:TPU:13, one launch (start us, length us, event | category | flops | bytes accessed | tf_op | source)
XLA Modules:
  0.0 364.2 jit_solution(4335219773419730291)
XLA Ops:
  0.6 8.9 %forward.7 = (f32[16,8,8,256]{3,2,1,0:T(8,128)}, f32[16,8,8,256]{3,2,1,0:T(8,128)}) custom-call(s32[2]{0:T(128)} %pad_add_fusion.half_ref, s32[2]{0:T(128)} %kweights_ref.7, s32[2,2]{1,0:T(2,128)} %occ_ref.7, bf16[2,2,2,32,256,256]{5,4,3,2,1,0:T(8,128)(2,1)} %orb_ref.7, bf16[256,256]{1,0:T(8,128)(2,1)} %constant.41.clone.yh_ref, ...), custom_call_target="tpu_custom_call" | custom-call | flops 1610612736 | bytes 12582912 | tf_op jit(solution)/shard_map/forward/pallas_call | solution.py:90
  10.7 8.9 %forward.5 = (f32[16,8,8,256]{3,2,1,0:T(8,128)}, f32[16,8,8,256]{3,2,1,0:T(8,128)}) custom-call(s32[2]{0:T(128)} %pad_add_fusion.half_ref, s32[2]{0:T(128)} %kweights_ref.7, s32[2,2]{1,0:T(2,128)} %occ_ref.7, bf16[2,2,2,32,256,256]{5,4,3,2,1,0:T(8,128)(2,1)} %orb_ref.7, bf16[256,256]{1,0:T(8,128)(2,1)} %constant.41.clone.yh_ref, ...), custom_call_target="tpu_custom_call" | custom-call | flops 1610612736 | bytes 12582912 | tf_op jit(solution)/shard_map/forward/pallas_call | solution.py:90
  19.9 9.0 %forward.6 = (f32[16,8,8,256]{3,2,1,0:T(8,128)}, f32[16,8,8,256]{3,2,1,0:T(8,128)}) custom-call(s32[2]{0:T(128)} %pad_add_fusion.half_ref, s32[2]{0:T(128)} %kweights_ref.7, s32[2,2]{1,0:T(2,128)} %occ_ref.7, bf16[2,2,2,32,256,256]{5,4,3,2,1,0:T(8,128)(2,1)} %orb_ref.7, bf16[256,256]{1,0:T(8,128)(2,1)} %constant.41.clone.yh_ref, ...), custom_call_target="tpu_custom_call" | custom-call | flops 1610612736 | bytes 12582912 | tf_op jit(solution)/shard_map/forward/pallas_call | solution.py:90
  30.1 9.0 %forward.4 = (f32[16,8,8,256]{3,2,1,0:T(8,128)}, f32[16,8,8,256]{3,2,1,0:T(8,128)}) custom-call(s32[2]{0:T(128)} %pad_add_fusion.half_ref, s32[2]{0:T(128)} %kweights_ref.7, s32[2,2]{1,0:T(2,128)} %occ_ref.7, bf16[2,2,2,32,256,256]{5,4,3,2,1,0:T(8,128)(2,1)} %orb_ref.7, bf16[256,256]{1,0:T(8,128)(2,1)} %constant.41.clone.yh_ref, ...), custom_call_target="tpu_custom_call" | custom-call | flops 1610612736 | bytes 12582912 | tf_op jit(solution)/shard_map/forward/pallas_call | solution.py:90
  41.7 7.6 %all-to-all-start = ((f32[16,8,8,256]{3,2,1,0:T(8,128)}), f32[16,8,8,256]{3,2,1,0:T(8,128)S(1)}, u32[]{:S(2)}, u32[]{:S(2)}) async-start(f32[16,8,8,256]{3,2,1,0:T(8,128)} %add.84), calls=%async_computation | async-start | bytes 2097152 | tf_op jit(solution)/shard_map/all_to_all | solution.py:316
  49.3 7.0 %collective-permute-done.14 = f32[16,8,8,256]{3,2,1,0:T(8,128)} collective-permute-done((f32[16,8,8,256]{3,2,1,0:T(8,128)}, f32[16,8,8,256]{3,2,1,0:T(8,128)}, u32[]{:S(2)}, u32[]{:S(2)}) %collective-permute-start.14) | collective-permute-done | bytes 1048608 | tf_op jit(solution)/shard_map/ppermute | solution.py:280
  62.2 16.6 %collective-permute-done.7 = f32[16,8,8,256]{3,2,1,0:T(8,128)} collective-permute-done((f32[16,8,8,256]{3,2,1,0:T(8,128)}, f32[16,8,8,256]{3,2,1,0:T(8,128)}, u32[]{:S(2)}, u32[]{:S(2)}) %collective-permute-start.7) | collective-permute-done | bytes 1048608 | tf_op jit(solution)/shard_map/ppermute | solution.py:280
  82.7 18.5 %collective-permute-done = f32[16,8,8,256]{3,2,1,0:T(8,128)S(1)} collective-permute-done((f32[16,8,8,256]{3,2,1,0:T(8,128)}, f32[16,8,8,256]{3,2,1,0:T(8,128)S(1)}, u32[]{:S(2)}, u32[]{:S(2)}) %collective-permute-start) | collective-permute-done | bytes 1048608 | tf_op jit(solution)/shard_map/ppermute | solution.py:280
  113.3 14.2 %collective-permute-done.9.refs_2_ = f32[4,8,8,256]{3,2,1,0:T(8,128)} collective-permute-done((f32[4,8,8,256]{3,2,1,0:T(8,128)}, f32[4,8,8,256]{3,2,1,0:T(8,128)}, u32[]{:S(2)}, u32[]{:S(2)}) %collective-permute-start.9) | collective-permute-done | bytes 262176 | tf_op jit(solution)/shard_map/ppermute | solution.py:285
  148.7 3.8 %prepare.1 = (bf16[4,128,512]{2,1,0:T(8,128)(2,1)}, bf16[4,128,512]{2,1,0:T(8,128)(2,1)}, bf16[4,512,128]{2,1,0:T(8,128)(2,1)}, bf16[4,512,128]{2,1,0:T(8,128)(2,1)}) custom-call(s32[2]{0:T(128)} %pad_add_fusion.half_ref, f32[16,32,512]{2,1,0:T(8,128)} %bitcast.4), custom_call_target="tpu_custom_call" | custom-call | flops 26214400 | bytes 3145728 | tf_op jit(solution)/shard_map/prepare/pallas_call | solution.py:122
  152.5 6.9 %project.3.refs_6_ = f32[8,512,256]{2,1,0:T(8,128)} custom-call(f32[4,8,8,256]{3,2,1,0:T(8,128)} %get-tuple-element.77.refs_0_, f32[4,8,8,256]{3,2,1,0:T(8,128)} %copy-done.18, f32[4,8,8,256]{3,2,1,0:T(8,128)} %copy-done.19, f32[4,8,8,256]{3,2,1,0:T(8,128)} %copy-done.21, bf16[4,512,128]{2,1,0:T(8,128)(2,1)} %get-tuple-element.67.refs_4_.refs_1_, ...), custom_call_target="tpu_custom_call" | custom-call | flops 805306368 | bytes 8388608 | tf_op jit(solution)/shard_map/project/pallas_call | solution.py:165
  162.5 6.2 %collective-permute-done.13.refs_3_ = f32[4,8,8,256]{3,2,1,0:T(8,128)S(1)} collective-permute-done((f32[4,8,8,256]{3,2,1,0:T(8,128)}, f32[4,8,8,256]{3,2,1,0:T(8,128)S(1)}, u32[]{:S(2)}, u32[]{:S(2)}) %collective-permute-start.13) | collective-permute-done | bytes 262176 | tf_op jit(solution)/shard_map/ppermute | solution.py:285
  169.4 8.2 %project.4.refs_6_ = f32[8,512,256]{2,1,0:T(8,128)} custom-call(f32[4,8,8,256]{3,2,1,0:T(8,128)} %get-tuple-element.71.refs_0_, f32[4,8,8,256]{3,2,1,0:T(8,128)} %copy-done.20, f32[4,8,8,256]{3,2,1,0:T(8,128)} %copy-done.25, f32[4,8,8,256]{3,2,1,0:T(8,128)} %copy-done.26, bf16[4,512,128]{2,1,0:T(8,128)(2,1)} %get-tuple-element.67.refs_4_.refs_1_, ...), custom_call_target="tpu_custom_call" | custom-call | flops 805306368 | bytes 8388608 | tf_op jit(solution)/shard_map/project/pallas_call | solution.py:165
  178.5 8.1 %project.5.part_ref = f32[8,512,256]{2,1,0:T(8,128)} custom-call(f32[4,8,8,256]{3,2,1,0:T(8,128)} %get-tuple-element.61.refs_0_, f32[4,8,8,256]{3,2,1,0:T(8,128)} %copy-done.22, f32[4,8,8,256]{3,2,1,0:T(8,128)} %copy-done.23, f32[4,8,8,256]{3,2,1,0:T(8,128)} %copy-done.24, bf16[4,512,128]{2,1,0:T(8,128)(2,1)} %get-tuple-element.67.refs_4_.refs_1_, ...), custom_call_target="tpu_custom_call" | custom-call | flops 805306368 | bytes 8388608 | tf_op jit(solution)/shard_map/project/pallas_call | solution.py:165
  187.6 9.3 %solve.1 = (f32[16,8,8,256]{3,2,1,0:T(8,128)}, bf16[8,512,256]{2,1,0:T(8,128)(2,1)}, bf16[8,512,256]{2,1,0:T(8,128)(2,1)}) custom-call(f32[8,512,256]{2,1,0:T(8,128)} %project.5.part_ref, f32[16,8,8,256]{3,2,1,0:T(8,128)} %copy-done, bf16[4,512,128]{2,1,0:T(8,128)(2,1)} %get-tuple-element.67.refs_4_.refs_1_, ...), custom_call_target="tpu_custom_call" | custom-call | flops 1610612736 | bytes 12582912 | tf_op jit(solution)/shard_map/solve/pallas_call | solution.py:192
  196.9 6.6 %all-to-all-start.1 = ((f32[16,8,8,256]{3,2,1,0:T(8,128)}), f32[16,8,8,256]{3,2,1,0:T(8,128)S(1)}, u32[]{:S(2)}, u32[]{:S(2)}) async-start(f32[16,8,8,256]{3,2,1,0:T(8,128)} %get-tuple-element.112), calls=%async_computation.1 | async-start | bytes 2097152 | tf_op jit(solution)/shard_map/all_to_all | solution.py:316
  203.5 6.8 %filtered.5 = (f32[4,8,8,256]{3,2,1,0:T(8,128)}, f32[4,8,8,256]{3,2,1,0:T(8,128)}, f32[4,8,8,256]{3,2,1,0:T(8,128)}, f32[4,8,8,256]{3,2,1,0:T(8,128)}) custom-call(bf16[8,512,256]{2,1,0:T(8,128)(2,1)} %get-tuple-element.86.wh_ref, bf16[8,512,256]{2,1,0:T(8,128)(2,1)} %get-tuple-element.87.wl_ref, bf16[4,128,512]{2,1,0:T(8,128)(2,1)} %get-tuple-element.83.refs_3_.zh_ref, ...), custom_call_target="tpu_custom_call" | custom-call | flops 805306368 | bytes 4194304 | tf_op jit(solution)/shard_map/filtered/pallas_call | solution.py:215
  212.5 6.8 %filtered.4 = (f32[4,8,8,256]{3,2,1,0:T(8,128)}, f32[4,8,8,256]{3,2,1,0:T(8,128)}, f32[4,8,8,256]{3,2,1,0:T(8,128)}, f32[4,8,8,256]{3,2,1,0:T(8,128)}) custom-call(bf16[8,512,256]{2,1,0:T(8,128)(2,1)} %get-tuple-element.86.wh_ref, bf16[8,512,256]{2,1,0:T(8,128)(2,1)} %get-tuple-element.87.wl_ref, bf16[4,128,512]{2,1,0:T(8,128)(2,1)} %get-tuple-element.83.refs_3_.zh_ref, ...), custom_call_target="tpu_custom_call" | custom-call | flops 805306368 | bytes 4194304 | tf_op jit(solution)/shard_map/filtered/pallas_call | solution.py:215
  219.7 6.7 %filtered.3 = (f32[4,8,8,256]{3,2,1,0:T(8,128)}, f32[4,8,8,256]{3,2,1,0:T(8,128)}, f32[4,8,8,256]{3,2,1,0:T(8,128)}, f32[4,8,8,256]{3,2,1,0:T(8,128)}) custom-call(bf16[8,512,256]{2,1,0:T(8,128)(2,1)} %get-tuple-element.86.wh_ref, bf16[8,512,256]{2,1,0:T(8,128)(2,1)} %get-tuple-element.87.wl_ref, bf16[4,128,512]{2,1,0:T(8,128)(2,1)} %get-tuple-element.83.refs_3_.zh_ref, ...), custom_call_target="tpu_custom_call" | custom-call | flops 805306368 | bytes 4194304 | tf_op jit(solution)/shard_map/filtered/pallas_call | solution.py:215
  232.0 3.6 collective-permute-done.33.refs_2_
  249.0 4.0 %collective-permute-done.24.refs_3_ = f32[4,8,8,256]{3,2,1,0:T(8,128)S(1)} collective-permute-done((f32[4,8,8,256]{3,2,1,0:T(8,128)}, f32[4,8,8,256]{3,2,1,0:T(8,128)S(1)}, u32[]{:S(2)}, u32[]{:S(2)}) %collective-permute-start.24) | collective-permute-done | bytes 262176 | tf_op jit(solution)/shard_map/ppermute | solution.py:285
  257.3 4.0 %collective-permute-done.46.refs_2_ = f32[4,8,8,256]{3,2,1,0:T(8,128)S(1)} collective-permute-done((f32[4,8,8,256]{3,2,1,0:T(8,128)}, f32[4,8,8,256]{3,2,1,0:T(8,128)S(1)}, u32[]{:S(2)}, u32[]{:S(2)}) %collective-permute-start.46) | collective-permute-done | bytes 262176 | tf_op jit(solution)/shard_map/ppermute | solution.py:285
  264.5 16.4 %collective-permute-done.47.refs_3_ = f32[4,8,8,256]{3,2,1,0:T(8,128)S(1)} collective-permute-done((f32[4,8,8,256]{3,2,1,0:T(8,128)}, f32[4,8,8,256]{3,2,1,0:T(8,128)S(1)}, u32[]{:S(2)}, u32[]{:S(2)}) %collective-permute-start.47) | collective-permute-done | bytes 262176 | tf_op jit(solution)/shard_map/ppermute | solution.py:285
  287.1 5.1 %collective-permute-done.37.refs_3_ = f32[4,8,8,256]{3,2,1,0:T(8,128)} collective-permute-done((f32[4,8,8,256]{3,2,1,0:T(8,128)}, f32[4,8,8,256]{3,2,1,0:T(8,128)}, u32[]{:S(2)}, u32[]{:S(2)}) %collective-permute-start.37) | collective-permute-done | bytes 262176 | tf_op jit(solution)/shard_map/ppermute | solution.py:285
  294.4 12.0 %collective-permute-done.26.refs_2_ = f32[4,8,8,256]{3,2,1,0:T(8,128)S(1)} collective-permute-done((f32[4,8,8,256]{3,2,1,0:T(8,128)}, f32[4,8,8,256]{3,2,1,0:T(8,128)S(1)}, u32[]{:S(2)}, u32[]{:S(2)}) %collective-permute-start.26) | collective-permute-done | bytes 262176 | tf_op jit(solution)/shard_map/ppermute | solution.py:285
  307.7 7.0 %collective-permute-done.27.refs_3_ = f32[4,8,8,256]{3,2,1,0:T(8,128)S(1)} collective-permute-done((f32[4,8,8,256]{3,2,1,0:T(8,128)}, f32[4,8,8,256]{3,2,1,0:T(8,128)S(1)}, u32[]{:S(2)}, u32[]{:S(2)}) %collective-permute-start.27) | collective-permute-done | bytes 262176 | tf_op jit(solution)/shard_map/ppermute | solution.py:285
  317.6 6.7 %inverse.4.refs_12_ = f32[32,256,256]{2,1,0:T(8,128)} custom-call(s32[2]{0:T(128)} %pad_add_fusion.half_ref, f32[16,8,8,256]{3,2,1,0:T(8,128)} %copy-done.1, f32[16,8,8,256]{3,2,1,0:T(8,128)} %copy-done.4, bf16[256,256]{1,0:T(8,128)(2,1)} %constant.45.clone.refs_2_.refs_8_, bf16[256,256]{1,0:T(8,128)(2,1)} %constant.46.clone.refs_3_.refs_9_, ...), custom_call_target="tpu_custom_call" | custom-call | flops 1610612736 | bytes 4194304 | tf_op jit(solution)/shard_map/inverse/pallas_call | solution.py:256
  330.0 6.8 %inverse.5.refs_12_ = f32[32,256,256]{2,1,0:T(8,128)} custom-call(s32[2]{0:T(128)} %pad_add_fusion.half_ref, f32[4,8,8,256]{3,2,1,0:T(8,128)} %get-tuple-element.108.refs_0_, f32[4,8,8,256]{3,2,1,0:T(8,128)} %copy-done.5, f32[4,8,8,256]{3,2,1,0:T(8,128)} %copy-done.6, f32[4,8,8,256]{3,2,1,0:T(8,128)} %copy-done.7, ...), custom_call_target="tpu_custom_call", output_to_operand_aliasing={{}: (13, {})} | custom-call | flops 1610612736 | bytes 4194304 | tf_op jit(solution)/shard_map/inverse/pallas_call | solution.py:256
  336.8 6.8 %inverse.6.refs_12_ = f32[32,256,256]{2,1,0:T(8,128)} custom-call(s32[2]{0:T(128)} %pad_add_fusion.half_ref, f32[4,8,8,256]{3,2,1,0:T(8,128)} %get-tuple-element.100.refs_0_, f32[4,8,8,256]{3,2,1,0:T(8,128)} %copy-done.9, f32[4,8,8,256]{3,2,1,0:T(8,128)} %collective-permute-done.36.refs_2_, ...), custom_call_target="tpu_custom_call", output_to_operand_aliasing={{}: (13, {})} | custom-call | flops 1610612736 | bytes 4194304 | tf_op jit(solution)/shard_map/inverse/pallas_call | solution.py:256
  345.5 5.6 %collective-permute-done.30.refs_6_ = f32[4,8,8,256]{3,2,1,0:T(8,128)S(1)} collective-permute-done((f32[4,8,8,256]{3,2,1,0:T(8,128)}, f32[4,8,8,256]{3,2,1,0:T(8,128)S(1)}, u32[]{:S(2)}, u32[]{:S(2)}) %collective-permute-start.30) | collective-permute-done | bytes 262176 | tf_op jit(solution)/shard_map/ppermute | solution.py:280
  351.1 5.6 %collective-permute-done.31.refs_7_ = f32[4,8,8,256]{3,2,1,0:T(8,128)S(1)} collective-permute-done((f32[4,8,8,256]{3,2,1,0:T(8,128)}, f32[4,8,8,256]{3,2,1,0:T(8,128)S(1)}, u32[]{:S(2)}, u32[]{:S(2)}) %collective-permute-start.31) | collective-permute-done | bytes 262176 | tf_op jit(solution)/shard_map/ppermute | solution.py:280
  357.4 6.8 %inverse.7 = f32[32,256,256]{2,1,0:T(8,128)} custom-call(s32[2]{0:T(128)} %pad_add_fusion.half_ref, f32[4,8,8,256]{3,2,1,0:T(8,128)} %get-tuple-element.92.refs_0_, f32[4,8,8,256]{3,2,1,0:T(8,128)} %copy-done.10, f32[4,8,8,256]{3,2,1,0:T(8,128)} %copy-done.11, f32[4,8,8,256]{3,2,1,0:T(8,128)} %copy-done.12, ...), custom_call_target="tpu_custom_call", output_to_operand_aliasing={{}: (13, {})} | custom-call | flops 1610612736 | bytes 4194304 | tf_op jit(solution)/shard_map/inverse/pallas_call | solution.py:256
  (193 shorter events, 104.1 us)
Async XLA Ops:
  9.5 29.9 %collective-permute-start.21 = (f32[16,8,8,256]{3,2,1,0:T(8,128)}, f32[16,8,8,256]{3,2,1,0:T(8,128)}, u32[]{:S(2)}, u32[]{:S(2)}) collective-permute-start(f32[16,8,8,256]{3,2,1,0:T(8,128)} %get-tuple-element.82), channel_id=1, source_target_pairs={{0,16},{16,0},{1,17},{17,1},{2,18},{18,2},{3,19},{19,3},{4,20},{20... | collective-permute-start | bytes 3145736 | tf_op jit(solution)/shard_map/ppermute | solution.py:280
  19.6 36.7 %collective-permute-start.14 = (f32[16,8,8,256]{3,2,1,0:T(8,128)}, f32[16,8,8,256]{3,2,1,0:T(8,128)}, u32[]{:S(2)}, u32[]{:S(2)}) collective-permute-start(f32[16,8,8,256]{3,2,1,0:T(8,128)} %get-tuple-element.76), channel_id=1, source_target_pairs={{0,16},{16,0},{1,17},{17,1},{2,18},{18,2},{3,19},{19,3},{4,20},{20... | collective-permute-start | bytes 3145736 | tf_op jit(solution)/shard_map/ppermute | solution.py:280
  28.9 49.9 %collective-permute-start.7 = (f32[16,8,8,256]{3,2,1,0:T(8,128)}, f32[16,8,8,256]{3,2,1,0:T(8,128)}, u32[]{:S(2)}, u32[]{:S(2)}) collective-permute-start(f32[16,8,8,256]{3,2,1,0:T(8,128)} %get-tuple-element.70), channel_id=1, source_target_pairs={{0,16},{16,0},{1,17},{17,1},{2,18},{18,2},{3,19},{19,3},{4,20},{20... | collective-permute-start | bytes 3145736 | tf_op jit(solution)/shard_map/ppermute | solution.py:280
  39.0 62.1 %collective-permute-start = (f32[16,8,8,256]{3,2,1,0:T(8,128)}, f32[16,8,8,256]{3,2,1,0:T(8,128)S(1)}, u32[]{:S(2)}, u32[]{:S(2)}) collective-permute-start(f32[16,8,8,256]{3,2,1,0:T(8,128)} %get-tuple-element.60), channel_id=1, source_target_pairs={{0,16},{16,0},{1,17},{17,1},{2,18},{18,2},{3,19},{19,3},{4,20},{20... | collective-permute-start | bytes 3145736 | tf_op jit(solution)/shard_map/ppermute | solution.py:280
  41.7 144.9 %all-to-all-start = ((f32[16,8,8,256]{3,2,1,0:T(8,128)}), f32[16,8,8,256]{3,2,1,0:T(8,128)S(1)}, u32[]{:S(2)}, u32[]{:S(2)}) async-start(f32[16,8,8,256]{3,2,1,0:T(8,128)} %add.84), calls=%async_computation | async-start | bytes 2097152 | tf_op jit(solution)/shard_map/all_to_all | solution.py:316
  58.7 44.8 %collective-permute-start.17 = (f32[4,8,8,256]{3,2,1,0:T(8,128)S(1)}, f32[4,8,8,256]{3,2,1,0:T(8,128)S(1)}, u32[]{:S(2)}, u32[]{:S(2)}) collective-permute-start(f32[4,8,8,256]{3,2,1,0:T(8,128)S(1)} %get-tuple-element.113), channel_id=1, source_target_pairs={{0,12},{1,13},{2,14},{3,15},{4,8},{5,9},{6,10},{7,11},{8,4},{9,5},... | collective-permute-start | bytes 786440 | tf_op jit(solution)/shard_map/ppermute | solution.py:285
  60.0 44.6 %collective-permute-start.16 = (f32[4,8,8,256]{3,2,1,0:T(8,128)S(1)}, f32[4,8,8,256]{3,2,1,0:T(8,128)S(1)}, u32[]{:S(2)}, u32[]{:S(2)}) collective-permute-start(f32[4,8,8,256]{3,2,1,0:T(8,128)S(1)} %get-tuple-element.114), channel_id=1, source_target_pairs={{0,8},{1,9},{2,10},{3,11},{4,12},{5,13},{6,14},{7,15},{8,0},{9,1},... | collective-permute-start | bytes 786440 | tf_op jit(solution)/shard_map/ppermute | solution.py:285
  61.0 43.8 %collective-permute-start.15 = (f32[4,8,8,256]{3,2,1,0:T(8,128)S(1)}, f32[4,8,8,256]{3,2,1,0:T(8,128)S(1)}, u32[]{:S(2)}, u32[]{:S(2)}) collective-permute-start(f32[4,8,8,256]{3,2,1,0:T(8,128)S(1)} %get-tuple-element.115), channel_id=1, source_target_pairs={{0,4},{1,5},{2,6},{3,7},{4,0},{5,1},{6,2},{7,3},{8,12},{9,13},{10,... | collective-permute-start | bytes 786440 | tf_op jit(solution)/shard_map/ppermute | solution.py:285
  81.4 32.0 %collective-permute-start.10 = (f32[4,8,8,256]{3,2,1,0:T(8,128)}, f32[4,8,8,256]{3,2,1,0:T(8,128)}, u32[]{:S(2)}, u32[]{:S(2)}) collective-permute-start(f32[4,8,8,256]{3,2,1,0:T(8,128)} %get-tuple-element.117), channel_id=1, source_target_pairs={{0,12},{1,13},{2,14},{3,15},{4,8},{5,9},{6,10},{7,11},{8,4},{9,5},... | collective-permute-start | bytes 786440 | tf_op jit(solution)/shard_map/ppermute | solution.py:285
  101.2 26.3 %collective-permute-start.9 = (f32[4,8,8,256]{3,2,1,0:T(8,128)}, f32[4,8,8,256]{3,2,1,0:T(8,128)}, u32[]{:S(2)}, u32[]{:S(2)}) collective-permute-start(f32[4,8,8,256]{3,2,1,0:T(8,128)} %get-tuple-element.118), channel_id=1, source_target_pairs={{0,8},{1,9},{2,10},{3,11},{4,12},{5,13},{6,14},{7,15},{8,0},{9,1},... | collective-permute-start | bytes 786440 | tf_op jit(solution)/shard_map/ppermute | solution.py:285
  103.5 26.4 %collective-permute-start.8 = (f32[4,8,8,256]{3,2,1,0:T(8,128)}, f32[4,8,8,256]{3,2,1,0:T(8,128)}, u32[]{:S(2)}, u32[]{:S(2)}) collective-permute-start(f32[4,8,8,256]{3,2,1,0:T(8,128)} %get-tuple-element.119), channel_id=1, source_target_pairs={{0,4},{1,5},{2,6},{3,7},{4,0},{5,1},{6,2},{7,3},{8,12},{9,13},{10,... | collective-permute-start | bytes 786440 | tf_op jit(solution)/shard_map/ppermute | solution.py:285
  104.6 31.1 %collective-permute-start.3 = (f32[4,8,8,256]{3,2,1,0:T(8,128)}, f32[4,8,8,256]{3,2,1,0:T(8,128)S(1)}, u32[]{:S(2)}, u32[]{:S(2)}) collective-permute-start(f32[4,8,8,256]{3,2,1,0:T(8,128)} %get-tuple-element.121), channel_id=1, source_target_pairs={{0,12},{1,13},{2,14},{3,15},{4,8},{5,9},{6,10},{7,11},{8,4},{9,5},... | collective-permute-start | bytes 786440 | tf_op jit(solution)/shard_map/ppermute | solution.py:285
  105.3 34.2 %collective-permute-start.2 = (f32[4,8,8,256]{3,2,1,0:T(8,128)}, f32[4,8,8,256]{3,2,1,0:T(8,128)S(1)}, u32[]{:S(2)}, u32[]{:S(2)}) collective-permute-start(f32[4,8,8,256]{3,2,1,0:T(8,128)} %get-tuple-element.122), channel_id=1, source_target_pairs={{0,8},{1,9},{2,10},{3,11},{4,12},{5,13},{6,14},{7,15},{8,0},{9,1},... | collective-permute-start | bytes 786440 | tf_op jit(solution)/shard_map/ppermute | solution.py:285
  113.3 27.3 %collective-permute-start.1 = (f32[4,8,8,256]{3,2,1,0:T(8,128)S(1)}, f32[4,8,8,256]{3,2,1,0:T(8,128)S(1)}, u32[]{:S(2)}, u32[]{:S(2)}) collective-permute-start(f32[4,8,8,256]{3,2,1,0:T(8,128)S(1)} %get-tuple-element.123), channel_id=1, source_target_pairs={{0,4},{1,5},{2,6},{3,7},{4,0},{5,1},{6,2},{7,3},{8,12},{9,13},{10,... | collective-permute-start | bytes 786440 | tf_op jit(solution)/shard_map/ppermute | solution.py:285
  143.5 34.1 %collective-permute-start.4 = (f32[4,8,8,256]{3,2,1,0:T(8,128)}, f32[4,8,8,256]{3,2,1,0:T(8,128)S(1)}, u32[]{:S(2)}, u32[]{:S(2)}) collective-permute-start(f32[4,8,8,256]{3,2,1,0:T(8,128)} %get-tuple-element.62), channel_id=1, source_target_pairs={{0,1},{1,0},{2,3},{3,2},{4,5},{5,4},{6,7},{7,6},{8,9},{9,8},{10,11... | collective-permute-start | bytes 786440 | tf_op jit(solution)/shard_map/ppermute | solution.py:285
  143.5 34.0 %collective-permute-start.5 = (f32[4,8,8,256]{3,2,1,0:T(8,128)}, f32[4,8,8,256]{3,2,1,0:T(8,128)S(1)}, u32[]{:S(2)}, u32[]{:S(2)}) collective-permute-start(f32[4,8,8,256]{3,2,1,0:T(8,128)} %get-tuple-element.63), channel_id=1, source_target_pairs={{0,2},{1,3},{2,0},{3,1},{4,6},{5,7},{6,4},{7,5},{8,10},{9,11},{10,... | collective-permute-start | bytes 786440 | tf_op jit(solution)/shard_map/ppermute | solution.py:285
  143.9 33.7 %collective-permute-start.6 = (f32[4,8,8,256]{3,2,1,0:T(8,128)}, f32[4,8,8,256]{3,2,1,0:T(8,128)S(1)}, u32[]{:S(2)}, u32[]{:S(2)}) collective-permute-start(f32[4,8,8,256]{3,2,1,0:T(8,128)} %get-tuple-element.64), channel_id=1, source_target_pairs={{0,3},{1,2},{2,1},{3,0},{4,7},{5,6},{6,5},{7,4},{8,11},{9,10},{10,... | collective-permute-start | bytes 786440 | tf_op jit(solution)/shard_map/ppermute | solution.py:285
  146.0 22.7 %collective-permute-start.13 = (f32[4,8,8,256]{3,2,1,0:T(8,128)}, f32[4,8,8,256]{3,2,1,0:T(8,128)S(1)}, u32[]{:S(2)}, u32[]{:S(2)}) collective-permute-start(f32[4,8,8,256]{3,2,1,0:T(8,128)} %get-tuple-element.74), channel_id=1, source_target_pairs={{0,3},{1,2},{2,1},{3,0},{4,7},{5,6},{6,5},{7,4},{8,11},{9,10},{10,... | collective-permute-start | bytes 786440 | tf_op jit(solution)/shard_map/ppermute | solution.py:285
  196.9 38.7 %all-to-all-start.1 = ((f32[16,8,8,256]{3,2,1,0:T(8,128)}), f32[16,8,8,256]{3,2,1,0:T(8,128)S(1)}, u32[]{:S(2)}, u32[]{:S(2)}) async-start(f32[16,8,8,256]{3,2,1,0:T(8,128)} %get-tuple-element.112), calls=%async_computation.1 | async-start | bytes 2097152 | tf_op jit(solution)/shard_map/all_to_all | solution.py:316
  231.6 21.4 %collective-permute-start.24 = (f32[4,8,8,256]{3,2,1,0:T(8,128)}, f32[4,8,8,256]{3,2,1,0:T(8,128)S(1)}, u32[]{:S(2)}, u32[]{:S(2)}) collective-permute-start(f32[4,8,8,256]{3,2,1,0:T(8,128)} %get-tuple-element.91), channel_id=1, source_target_pairs={{0,3},{1,2},{2,1},{3,0},{4,7},{5,6},{6,5},{7,4},{8,11},{9,10},{10,... | collective-permute-start | bytes 786440 | tf_op jit(solution)/shard_map/ppermute | solution.py:285
  235.6 80.6 %collective-permute-start.52 = (f32[16,8,8,256]{3,2,1,0:T(8,128)S(1)}, f32[16,8,8,256]{3,2,1,0:T(8,128)S(1)}, u32[]{:S(2)}, u32[]{:S(2)}) collective-permute-start(f32[16,8,8,256]{3,2,1,0:T(8,128)S(1)} %all-to-all-done.1.refs_0_), channel_id=1, source_target_pairs={{0,16},{16,0},{1,17},{17,1},{2,18},{18,2},{3,19},{19,3},{4,20},{20... | collective-permute-start | bytes 3145736 | tf_op jit(solution)/shard_map/ppermute | solution.py:280
  247.5 33.4 %collective-permute-start.47 = (f32[4,8,8,256]{3,2,1,0:T(8,128)}, f32[4,8,8,256]{3,2,1,0:T(8,128)S(1)}, u32[]{:S(2)}, u32[]{:S(2)}) collective-permute-start(f32[4,8,8,256]{3,2,1,0:T(8,128)} %get-tuple-element.111), channel_id=1, source_target_pairs={{0,12},{1,13},{2,14},{3,15},{4,8},{5,9},{6,10},{7,11},{8,4},{9,5},... | collective-permute-start | bytes 786440 | tf_op jit(solution)/shard_map/ppermute | solution.py:285
  253.7 27.2 %collective-permute-start.48 = (f32[4,8,8,256]{3,2,1,0:T(8,128)}, f32[4,8,8,256]{3,2,1,0:T(8,128)S(1)}, u32[]{:S(2)}, u32[]{:S(2)}) collective-permute-start(f32[4,8,8,256]{3,2,1,0:T(8,128)} %get-tuple-element.108.refs_0_), channel_id=1, source_target_pairs={{0,16},{16,0},{1,17},{17,1},{2,18},{18,2},{3,19},{19,3},{4,20},{20... | collective-permute-start | bytes 786440 | tf_op jit(solution)/shard_map/ppermute | solution.py:280
  257.1 27.2 %collective-permute-start.35 = (f32[4,8,8,256]{3,2,1,0:T(8,128)}, f32[4,8,8,256]{3,2,1,0:T(8,128)S(1)}, u32[]{:S(2)}, u32[]{:S(2)}) collective-permute-start(f32[4,8,8,256]{3,2,1,0:T(8,128)} %get-tuple-element.101), channel_id=1, source_target_pairs={{0,4},{1,5},{2,6},{3,7},{4,0},{5,1},{6,2},{7,3},{8,12},{9,13},{10,... | collective-permute-start | bytes 786440 | tf_op jit(solution)/shard_map/ppermute | solution.py:285
  261.2 23.2 %collective-permute-start.36 = (f32[4,8,8,256]{3,2,1,0:T(8,128)}, f32[4,8,8,256]{3,2,1,0:T(8,128)}, u32[]{:S(2)}, u32[]{:S(2)}) collective-permute-start(f32[4,8,8,256]{3,2,1,0:T(8,128)} %get-tuple-element.102), channel_id=1, source_target_pairs={{0,8},{1,9},{2,10},{3,11},{4,12},{5,13},{6,14},{7,15},{8,0},{9,1},... | collective-permute-start | bytes 786440 | tf_op jit(solution)/shard_map/ppermute | solution.py:285
  284.4 22.0 %collective-permute-start.26 = (f32[4,8,8,256]{3,2,1,0:T(8,128)}, f32[4,8,8,256]{3,2,1,0:T(8,128)S(1)}, u32[]{:S(2)}, u32[]{:S(2)}) collective-permute-start(f32[4,8,8,256]{3,2,1,0:T(8,128)} %get-tuple-element.94), channel_id=1, source_target_pairs={{0,8},{1,9},{2,10},{3,11},{4,12},{5,13},{6,14},{7,15},{8,0},{9,1},... | collective-permute-start | bytes 786440 | tf_op jit(solution)/shard_map/ppermute | solution.py:285
  292.2 22.5 %collective-permute-start.27 = (f32[4,8,8,256]{3,2,1,0:T(8,128)}, f32[4,8,8,256]{3,2,1,0:T(8,128)S(1)}, u32[]{:S(2)}, u32[]{:S(2)}) collective-permute-start(f32[4,8,8,256]{3,2,1,0:T(8,128)} %get-tuple-element.95), channel_id=1, source_target_pairs={{0,12},{1,13},{2,14},{3,15},{4,8},{5,9},{6,10},{7,11},{8,4},{9,5},... | collective-permute-start | bytes 786440 | tf_op jit(solution)/shard_map/ppermute | solution.py:285
  292.3 23.6 %collective-permute-start.49 = (f32[4,8,8,256]{3,2,1,0:T(8,128)S(1)}, f32[4,8,8,256]{3,2,1,0:T(8,128)S(1)}, u32[]{:S(2)}, u32[]{:S(2)}) collective-permute-start(f32[4,8,8,256]{3,2,1,0:T(8,128)S(1)} %collective-permute-done.45.refs_1_), channel_id=1, source_target_pairs={{0,16},{16,0},{1,17},{17,1},{2,18},{18,2},{3,19},{19,3},{4,20},{20... | collective-permute-start | bytes 786440 | tf_op jit(solution)/shard_map/ppermute | solution.py:280
  294.4 30.0 %collective-permute-start.50 = (f32[4,8,8,256]{3,2,1,0:T(8,128)S(1)}, f32[4,8,8,256]{3,2,1,0:T(8,128)}, u32[]{:S(2)}, u32[]{:S(2)}) collective-permute-start(f32[4,8,8,256]{3,2,1,0:T(8,128)S(1)} %collective-permute-done.46.refs_2_), channel_id=1, source_target_pairs={{0,16},{16,0},{1,17},{17,1},{2,18},{18,2},{3,19},{19,3},{4,20},{20... | collective-permute-start | bytes 786440 | tf_op jit(solution)/shard_map/ppermute | solution.py:280
  325.1 20.3 %collective-permute-start.29 = (f32[4,8,8,256]{3,2,1,0:T(8,128)}, f32[4,8,8,256]{3,2,1,0:T(8,128)S(1)}, u32[]{:S(2)}, u32[]{:S(2)}) collective-permute-start(f32[4,8,8,256]{3,2,1,0:T(8,128)} %copy-done.10), channel_id=1, source_target_pairs={{0,16},{16,0},{1,17},{17,1},{2,18},{18,2},{3,19},{19,3},{4,20},{20... | collective-permute-start | bytes 786440 | tf_op jit(solution)/shard_map/ppermute | solution.py:280
  325.8 25.3 %collective-permute-start.30 = (f32[4,8,8,256]{3,2,1,0:T(8,128)}, f32[4,8,8,256]{3,2,1,0:T(8,128)S(1)}, u32[]{:S(2)}, u32[]{:S(2)}) collective-permute-start(f32[4,8,8,256]{3,2,1,0:T(8,128)} %copy-done.11), channel_id=1, source_target_pairs={{0,16},{16,0},{1,17},{17,1},{2,18},{18,2},{3,19},{19,3},{4,20},{20... | collective-permute-start | bytes 786440 | tf_op jit(solution)/shard_map/ppermute | solution.py:280
  328.7 28.0 %collective-permute-start.31 = (f32[4,8,8,256]{3,2,1,0:T(8,128)}, f32[4,8,8,256]{3,2,1,0:T(8,128)S(1)}, u32[]{:S(2)}, u32[]{:S(2)}) collective-permute-start(f32[4,8,8,256]{3,2,1,0:T(8,128)} %copy-done.12), channel_id=1, source_target_pairs={{0,16},{16,0},{1,17},{17,1},{2,18},{18,2},{3,19},{19,3},{4,20},{20... | collective-permute-start | bytes 786440 | tf_op jit(solution)/shard_map/ppermute | solution.py:280
  (65 other events, 1077.3 us)

commit v3 on v2

--- a/solution.py
+++ b/solution.py
@@ -115,15 +115,15 @@
             return jnp.concatenate([z_ref[place] for place in places], axis=0)
 
         zh_ref[0], zl_ref[0] = split(rows_of(here == 0))
-        th_ref[0], tl_ref[0] = split(rows_of(here == chunks - 1).T)
+        th_ref[...], tl_ref[...] = split(rows_of(here == chunks - 1).T)
 
     straight = jax.ShapeDtypeStruct((chunks, size, nz), bf16)
-    turned = jax.ShapeDtypeStruct((chunks, nz, size), bf16)
+    turned = jax.ShapeDtypeStruct((nz, chunks * size), bf16)
     return pl.pallas_call(
         body,
         grid=(chunks,),
         in_specs=[smem(), pl.BlockSpec((blocks, GROUP, nz), lambda i: (0, i, 0))],
-        out_specs=[pl.BlockSpec((1, size, nz), lambda i: (i, 0, 0))] * 2 + [pl.BlockSpec((1, nz, size), lambda i: (i, 0, 0))] * 2,
+        out_specs=[pl.BlockSpec((1, size, nz), lambda i: (i, 0, 0))] * 2 + [pl.BlockSpec((nz, size), lambda i: (0, i))] * 2,
         out_shape=[straight] * 2 + [turned] * 2,
         cost_estimate=cost(nz * nz * 100, nz * nz * 12),
         name="prepare",
@@ -150,22 +150,23 @@
     return pl.BlockSpec((1,) + table.shape[1:], lambda i: (chunk, 0, 0))
 
 
-def project(columns, turned, chunk, before):
+def project(columns, turned, start, span, before):
     rows, _, ny = columns[0].shape[1:]
-    nz, size = turned[0].shape[1:]
+    nz = turned[0].shape[0]
+    size = sum(c.shape[0] for c in columns) * GROUP
     many = len(columns)
     extra = () if before is None else (before,)
 
     def body(*refs):
         xh, xl = split(gather_row(refs[:many], ny))
-        value = dot3(refs[many][0], refs[many + 1][0], xh, xl)
+        value = dot3(refs[many][...], refs[many + 1][...], xh, xl)
         refs[-1][0] = value if before is None else value + refs[many + 2][0]
 
     part = pl.BlockSpec((1, nz, ny), lambda i: (i, 0, 0))
     return pl.pallas_call(
         body,
         grid=(rows,),
-        in_specs=[by_row(c) for c in columns] + [one_chunk(t, chunk) for t in turned] + [part for _ in extra],
+        in_specs=[by_row(c) for c in columns] + [pl.BlockSpec((nz, size), lambda i: (0, start // span)) for _ in turned] + [part for _ in extra],
         out_specs=part,
         out_shape=jax.ShapeDtypeStruct((rows, nz, ny), f32),
         cost_estimate=cost(6 * nz * size * rows * ny, 8 * nz * rows * ny),
@@ -173,16 +174,17 @@
     )(*columns, *turned, *extra)
 
 
-def solve(part, columns, straight, turned, eigen, shift, chunk):
+def solve(part, columns, straight, turned, eigen, shift, start, span):
     rows, _, ny = columns[0].shape[1:]
-    nz, size = turned[0].shape[1:]
+    nz = turned[0].shape[0]
+    size = sum(c.shape[0] for c in columns) * GROUP
     many = len(columns)
 
     def body(part_ref, *refs):
         th_ref, tl_ref, zh_ref, zl_ref, e_ref, s_ref = refs[many : many + 6]
         wh_ref, wl_ref = refs[-2:]
         xh, xl = split(gather_row(refs[:many], ny))
-        projected = part_ref[0] + dot3(th_ref[0], tl_ref[0], xh, xl)
+        projected = part_ref[0] + dot3(th_ref[...], tl_ref[...], xh, xl)
         wh, wl = split(projected / (e_ref[...] + s_ref[0]))
         wh_ref[0], wl_ref[0] = wh, wl
         scatter_row(refs[many + 6 : -2], dot3(zh_ref[0], zl_ref[0], wh, wl))
@@ -194,11 +196,11 @@
         grid=(rows,),
         in_specs=[w_spec]
         + [by_row(c) for c in columns]
-        + [one_chunk(t, chunk) for t in turned]
+        + [pl.BlockSpec((nz, size), lambda i: (0, start // span)) for _ in turned]
         + [one_chunk(z, 0) for z in straight]
         + [whole(eigen.shape), pl.BlockSpec((1, 1, ny), lambda i: (i, 0, 0))],
-        out_specs=[by_row(c) for c in columns] + [w_spec, w_spec],
-        out_shape=[jax.ShapeDtypeStruct(c.shape, f32) for c in columns] + [w_shape, w_shape],
+        out_specs=[by_row(columns[-1]), w_spec, w_spec],
+        out_shape=[jax.ShapeDtypeStruct(columns[-1].shape, f32), w_shape, w_shape],
         cost_estimate=cost(12 * nz * rows * ny * size, 12 * nz * rows * ny),
         name="solve",
     )(part, *columns, *turned, *straight, eigen, shift)
@@ -347,11 +349,12 @@
     first = (mine * blocks + lax.axis_index("grid")) * rows
     shift = row_shift(first, rows, nx, ny)[:, None, :]
     part = None
-    for chunk in range(chunks - 1):
-        part = project(columns[chunk], (th, tl), chunk, part)
+    tail = 2 - chunks % 2
+    for chunk in range(0, chunks - tail, 2):
+        part = project(columns[chunk] + columns[chunk + 1], (th, tl), chunk, 2, part)
     if part is None:
         part = jnp.zeros((rows, planes * blocks, ny), f32)
-    ready, wh, wl = solve(part, columns[-1], (zh, zl), (th, tl), z_eigen[:, None], shift, chunks - 1)
+    ready, wh, wl = solve(part, sum(columns[-tail:], []), (zh, zl), (th, tl), z_eigen[:, None], shift, chunks - tail, tail)
     out = None
     for chunk in range(chunks):
         if chunk == 0:

time: 369 us -> 349 us (0.946)
  Pallas kernels: 133 us -> 117 us
  waiting for transfers between devices: 149 us -> 143 us
  starting transfers between devices: 64.2 us -> 69.3 us
    pallas_call x3 -> x1, Pallas kernels: 23.2 us -> 7.41 us  [project(): pl.pallas_call(body, grid=(rows,), in_specs=[by_row(c) for c in columns]...]
    ppermute x36, waiting for transfers between devices: 92 us -> 85.3 us  [pairwise(): lax.ppermute(value, 'grid', [(place, place ^ distance) for place in range...]
    ppermute x36, starting transfers between devices: 34.1 us -> 39.4 us  [pairwise(): lax.ppermute(value, 'grid', [(place, place ^ distance) for place in range...]
  transfers between devices with their start and end apart: 55 -> 55, of which waited for: 23 -> 22; matrix products, arithmetic and copies ran while one was open for 3% -> 3% of each run, Pallas kernels for 30% -> 27%
where the time goes in v3:
time: 349 us; the launch traced here: 345 us
  waiting for transfers between devices  143 us (41%)
  Pallas kernels  117 us (34%)
  starting transfers between devices  69.3 us (20%)
  other arithmetic  9.61 us (3%)
  local copies, waits for them, and re-layouts  5.67 us (2%)
    ppermute x36, waiting for transfers between devices, pairwise(): lax.ppermute(value, 'grid', [(place, place ^ distance) for place in range...  85.3 us
    ppermute x17, waiting for transfers between devices, swap(): return lax.ppermute(value, 'kpt', [(0, 1), (1, 0)])  57.4 us
    ppermute x36, starting transfers between devices, pairwise(): lax.ppermute(value, 'grid', [(place, place ^ distance) for place in range...  39.4 us
    pallas_call x4, Pallas kernels, forward(): pl.pallas_call(body, grid=(steps,), in_specs=[smem(), smem(), smem()] + [...  35.9 us
    pallas_call x4, Pallas kernels, inverse(): pl.pallas_call(body, grid=(steps,), in_specs=[smem()] + [whole(v.shape) f...  27.1 us
    pallas_call x3, Pallas kernels, filtered(): pl.pallas_call(body, grid=(rows,), in_specs=[w_spec, w_spec] + [one_chunk...  20.3 us
    ppermute x17, starting transfers between devices, swap(): return lax.ppermute(value, 'kpt', [(0, 1), (1, 0)])  15.7 us
    all_to_all x2, starting transfers between devices, exchange(): lax.all_to_all(value, 'grid', split_axis=0, concat_axis=0, tiled=True)  14.1 us
  transfers between devices with their start and end apart: 55, of which 22 were waited for; matrix products, arithmetic and copies ran while one was open for 3% of the time, Pallas kernels for 27%

profile of v3, /device:TPU:13, one launch (start us, length us, event | category | flops | bytes accessed | tf_op | source)
XLA Modules:
  0.0 344.8 jit_solution(5372519154931231311)
XLA Ops:
  0.6 8.9 %forward.7 = (f32[16,8,8,256]{3,2,1,0:T(8,128)}, f32[16,8,8,256]{3,2,1,0:T(8,128)}) custom-call(s32[2]{0:T(128)} %pad_add_fusion.half_ref, s32[2]{0:T(128)} %kweights_ref.7, s32[2,2]{1,0:T(2,128)} %occ_ref.7, bf16[2,2,2,32,256,256]{5,4,3,2,1,0:T(8,128)(2,1)} %orb_ref.7, bf16[256,256]{1,0:T(8,128)(2,1)} %constant.41.clone.yh_ref, ...), custom_call_target="tpu_custom_call" | custom-call | flops 1610612736 | bytes 12582912 | tf_op jit(solution)/shard_map/forward/pallas_call | solution.py:90
  10.8 9.0 %forward.5 = (f32[16,8,8,256]{3,2,1,0:T(8,128)}, f32[16,8,8,256]{3,2,1,0:T(8,128)}) custom-call(s32[2]{0:T(128)} %pad_add_fusion.half_ref, s32[2]{0:T(128)} %kweights_ref.7, s32[2,2]{1,0:T(2,128)} %occ_ref.7, bf16[2,2,2,32,256,256]{5,4,3,2,1,0:T(8,128)(2,1)} %orb_ref.7, bf16[256,256]{1,0:T(8,128)(2,1)} %constant.41.clone.yh_ref, ...), custom_call_target="tpu_custom_call" | custom-call | flops 1610612736 | bytes 12582912 | tf_op jit(solution)/shard_map/forward/pallas_call | solution.py:90
  20.1 9.0 %forward.4 = (f32[16,8,8,256]{3,2,1,0:T(8,128)}, f32[16,8,8,256]{3,2,1,0:T(8,128)}) custom-call(s32[2]{0:T(128)} %pad_add_fusion.half_ref, s32[2]{0:T(128)} %kweights_ref.7, s32[2,2]{1,0:T(2,128)} %occ_ref.7, bf16[2,2,2,32,256,256]{5,4,3,2,1,0:T(8,128)(2,1)} %orb_ref.7, bf16[256,256]{1,0:T(8,128)(2,1)} %constant.41.clone.yh_ref, ...), custom_call_target="tpu_custom_call" | custom-call | flops 1610612736 | bytes 12582912 | tf_op jit(solution)/shard_map/forward/pallas_call | solution.py:90
  30.2 9.0 %forward.6 = (f32[16,8,8,256]{3,2,1,0:T(8,128)}, f32[16,8,8,256]{3,2,1,0:T(8,128)}) custom-call(s32[2]{0:T(128)} %pad_add_fusion.half_ref, s32[2]{0:T(128)} %kweights_ref.7, s32[2,2]{1,0:T(2,128)} %occ_ref.7, bf16[2,2,2,32,256,256]{5,4,3,2,1,0:T(8,128)(2,1)} %orb_ref.7, bf16[256,256]{1,0:T(8,128)(2,1)} %constant.41.clone.yh_ref, ...), custom_call_target="tpu_custom_call" | custom-call | flops 1610612736 | bytes 12582912 | tf_op jit(solution)/shard_map/forward/pallas_call | solution.py:90
  42.4 7.5 %all-to-all-start = ((f32[16,8,8,256]{3,2,1,0:T(8,128)}), f32[16,8,8,256]{3,2,1,0:T(8,128)}, u32[]{:S(2)}, u32[]{:S(2)}) async-start(f32[16,8,8,256]{3,2,1,0:T(8,128)} %add.84), calls=%async_computation | async-start | bytes 2097152 | tf_op jit(solution)/shard_map/all_to_all | solution.py:318
  49.9 6.5 %collective-permute-done.7 = f32[16,8,8,256]{3,2,1,0:T(8,128)} collective-permute-done((f32[16,8,8,256]{3,2,1,0:T(8,128)}, f32[16,8,8,256]{3,2,1,0:T(8,128)}, u32[]{:S(2)}, u32[]{:S(2)}) %collective-permute-start.7) | collective-permute-done | bytes 1048608 | tf_op jit(solution)/shard_map/ppermute | solution.py:282
  62.3 16.6 %collective-permute-done = f32[16,8,8,256]{3,2,1,0:T(8,128)} collective-permute-done((f32[16,8,8,256]{3,2,1,0:T(8,128)}, f32[16,8,8,256]{3,2,1,0:T(8,128)}, u32[]{:S(2)}, u32[]{:S(2)}) %collective-permute-start) | collective-permute-done | bytes 1048608 | tf_op jit(solution)/shard_map/ppermute | solution.py:282
  82.3 18.9 %collective-permute-done.14 = f32[16,8,8,256]{3,2,1,0:T(8,128)S(1)} collective-permute-done((f32[16,8,8,256]{3,2,1,0:T(8,128)}, f32[16,8,8,256]{3,2,1,0:T(8,128)S(1)}, u32[]{:S(2)}, u32[]{:S(2)}) %collective-permute-start.14) | collective-permute-done | bytes 1048608 | tf_op jit(solution)/shard_map/ppermute | solution.py:282
  110.2 3.7 %collective-permute-done.3.refs_3_ = f32[4,8,8,256]{3,2,1,0:T(8,128)} collective-permute-done((f32[4,8,8,256]{3,2,1,0:T(8,128)}, f32[4,8,8,256]{3,2,1,0:T(8,128)}, u32[]{:S(2)}, u32[]{:S(2)}) %collective-permute-start.3) | collective-permute-done | bytes 262176 | tf_op jit(solution)/shard_map/ppermute | solution.py:287
  113.9 14.7 %collective-permute-done.2.refs_2_ = f32[4,8,8,256]{3,2,1,0:T(8,128)} collective-permute-done((f32[4,8,8,256]{3,2,1,0:T(8,128)}, f32[4,8,8,256]{3,2,1,0:T(8,128)}, u32[]{:S(2)}, u32[]{:S(2)}) %collective-permute-start.2) | collective-permute-done | bytes 262176 | tf_op jit(solution)/shard_map/ppermute | solution.py:287
  132.9 3.4 collective-permute-done.17.refs_3_
  149.8 3.9 %prepare.1 = (bf16[4,128,512]{2,1,0:T(8,128)(2,1)}, bf16[4,128,512]{2,1,0:T(8,128)(2,1)}, bf16[512,512]{1,0:T(8,128)(2,1)}, bf16[512,512]{1,0:T(8,128)(2,1)}) custom-call(s32[2]{0:T(128)} %pad_add_fusion.half_ref, f32[16,32,512]{2,1,0:T(8,128)} %bitcast.4), custom_call_target="tpu_custom_call" | custom-call | flops 26214400 | bytes 3145728 | tf_op jit(solution)/shard_map/prepare/pallas_call | solution.py:122
  156.5 7.4 %project.1.part_ref = f32[8,512,256]{2,1,0:T(8,128)} custom-call(f32[4,8,8,256]{3,2,1,0:T(8,128)} %get-tuple-element.62.refs_0_, f32[4,8,8,256]{3,2,1,0:T(8,128)} %copy-done.20, f32[4,8,8,256]{3,2,1,0:T(8,128)} %copy-done.21, f32[4,8,8,256]{3,2,1,0:T(8,128)} %copy-done.22, f32[4,8,8,256]{3,2,1,0:T(8,128)} %get-tuple-element.68.refs_4_, ...), custom_call_target="tpu_custom_call" | custom-call | flops 1610612736 | bytes 8388608 | tf_op jit(solution)/shard_map/project/pallas_call | solution.py:166
  167.7 9.8 %solve.1 = (f32[16,8,8,256]{3,2,1,0:T(8,128)}, bf16[8,512,256]{2,1,0:T(8,128)(2,1)}, bf16[8,512,256]{2,1,0:T(8,128)(2,1)}) custom-call(f32[8,512,256]{2,1,0:T(8,128)} %project.1.part_ref, f32[4,8,8,256]{3,2,1,0:T(8,128)} %get-tuple-element.77.refs_0_, f32[4,8,8,256]{3,2,1,0:T(8,128)} %copy-done.38, f32[4,8,8,256]{3,2,1,0:T(8,128)} %copy-done.39, ...), custom_call_target="tpu_custom_call" | custom-call | flops 3221225472 | bytes 12582912 | tf_op jit(solution)/shard_map/solve/pallas_call | solution.py:194
  177.5 6.6 %all-to-all-start.1 = ((f32[16,8,8,256]{3,2,1,0:T(8,128)}), f32[16,8,8,256]{3,2,1,0:T(8,128)S(1)}, u32[]{:S(2)}, u32[]{:S(2)}) async-start(f32[16,8,8,256]{3,2,1,0:T(8,128)} %get-tuple-element.112), calls=%async_computation.1 | async-start | bytes 2097152 | tf_op jit(solution)/shard_map/all_to_all | solution.py:318
  184.2 6.8 %filtered.5 = (f32[4,8,8,256]{3,2,1,0:T(8,128)}, f32[4,8,8,256]{3,2,1,0:T(8,128)}, f32[4,8,8,256]{3,2,1,0:T(8,128)}, f32[4,8,8,256]{3,2,1,0:T(8,128)}) custom-call(bf16[8,512,256]{2,1,0:T(8,128)(2,1)} %get-tuple-element.86.wh_ref, bf16[8,512,256]{2,1,0:T(8,128)(2,1)} %get-tuple-element.87.wl_ref, bf16[4,128,512]{2,1,0:T(8,128)(2,1)} %get-tuple-element.83.refs_7_.zh_ref, ...), custom_call_target="tpu_custom_call" | custom-call | flops 805306368 | bytes 4194304 | tf_op jit(solution)/shard_map/filtered/pallas_call | solution.py:217
  193.1 6.8 %filtered.4 = (f32[4,8,8,256]{3,2,1,0:T(8,128)}, f32[4,8,8,256]{3,2,1,0:T(8,128)}, f32[4,8,8,256]{3,2,1,0:T(8,128)}, f32[4,8,8,256]{3,2,1,0:T(8,128)}) custom-call(bf16[8,512,256]{2,1,0:T(8,128)(2,1)} %get-tuple-element.86.wh_ref, bf16[8,512,256]{2,1,0:T(8,128)(2,1)} %get-tuple-element.87.wl_ref, bf16[4,128,512]{2,1,0:T(8,128)(2,1)} %get-tuple-element.83.refs_7_.zh_ref, ...), custom_call_target="tpu_custom_call" | custom-call | flops 805306368 | bytes 4194304 | tf_op jit(solution)/shard_map/filtered/pallas_call | solution.py:217
  200.3 6.7 %filtered.3 = (f32[4,8,8,256]{3,2,1,0:T(8,128)}, f32[4,8,8,256]{3,2,1,0:T(8,128)}, f32[4,8,8,256]{3,2,1,0:T(8,128)}, f32[4,8,8,256]{3,2,1,0:T(8,128)}) custom-call(bf16[8,512,256]{2,1,0:T(8,128)(2,1)} %get-tuple-element.86.wh_ref, bf16[8,512,256]{2,1,0:T(8,128)(2,1)} %get-tuple-element.87.wl_ref, bf16[4,128,512]{2,1,0:T(8,128)(2,1)} %get-tuple-element.83.refs_7_.zh_ref, ...), custom_call_target="tpu_custom_call" | custom-call | flops 805306368 | bytes 4194304 | tf_op jit(solution)/shard_map/filtered/pallas_call | solution.py:217
  212.6 3.6 %collective-permute-done.33.refs_2_ = f32[4,8,8,256]{3,2,1,0:T(8,128)S(1)} collective-permute-done((f32[4,8,8,256]{3,2,1,0:T(8,128)}, f32[4,8,8,256]{3,2,1,0:T(8,128)S(1)}, u32[]{:S(2)}, u32[]{:S(2)}) %collective-permute-start.33) | collective-permute-done | bytes 262176 | tf_op jit(solution)/shard_map/ppermute | solution.py:287
  219.6 3.4 collective-permute-done.34.refs_3_
  229.6 4.1 %collective-permute-done.24.refs_3_ = f32[4,8,8,256]{3,2,1,0:T(8,128)S(1)} collective-permute-done((f32[4,8,8,256]{3,2,1,0:T(8,128)}, f32[4,8,8,256]{3,2,1,0:T(8,128)S(1)}, u32[]{:S(2)}, u32[]{:S(2)}) %collective-permute-start.24) | collective-permute-done | bytes 262176 | tf_op jit(solution)/shard_map/ppermute | solution.py:287
  237.9 7.3 %collective-permute-start.36 = (f32[4,8,8,256]{3,2,1,0:T(8,128)}, f32[4,8,8,256]{3,2,1,0:T(8,128)}, u32[]{:S(2)}, u32[]{:S(2)}) collective-permute-start(f32[4,8,8,256]{3,2,1,0:T(8,128)} %get-tuple-element.102), channel_id=1, source_target_pairs={{0,8},{1,9},{2,10},{3,11},{4,12},{5,13},{6,14},{7,15},{8,0},{9,1},... | collective-permute-start | bytes 786440 | tf_op jit(solution)/shard_map/ppermute | solution.py:287
  245.1 16.4 %collective-permute-done.47.refs_3_ = f32[4,8,8,256]{3,2,1,0:T(8,128)S(1)} collective-permute-done((f32[4,8,8,256]{3,2,1,0:T(8,128)}, f32[4,8,8,256]{3,2,1,0:T(8,128)S(1)}, u32[]{:S(2)}, u32[]{:S(2)}) %collective-permute-start.47) | collective-permute-done | bytes 262176 | tf_op jit(solution)/shard_map/ppermute | solution.py:287
  267.7 5.1 %collective-permute-done.37.refs_3_ = f32[4,8,8,256]{3,2,1,0:T(8,128)} collective-permute-done((f32[4,8,8,256]{3,2,1,0:T(8,128)}, f32[4,8,8,256]{3,2,1,0:T(8,128)}, u32[]{:S(2)}, u32[]{:S(2)}) %collective-permute-start.37) | collective-permute-done | bytes 262176 | tf_op jit(solution)/shard_map/ppermute | solution.py:287
  275.0 12.1 %collective-permute-done.26.refs_2_ = f32[4,8,8,256]{3,2,1,0:T(8,128)S(1)} collective-permute-done((f32[4,8,8,256]{3,2,1,0:T(8,128)}, f32[4,8,8,256]{3,2,1,0:T(8,128)S(1)}, u32[]{:S(2)}, u32[]{:S(2)}) %collective-permute-start.26) | collective-permute-done | bytes 262176 | tf_op jit(solution)/shard_map/ppermute | solution.py:287
  288.3 7.0 %collective-permute-done.27.refs_3_ = f32[4,8,8,256]{3,2,1,0:T(8,128)S(1)} collective-permute-done((f32[4,8,8,256]{3,2,1,0:T(8,128)}, f32[4,8,8,256]{3,2,1,0:T(8,128)S(1)}, u32[]{:S(2)}, u32[]{:S(2)}) %collective-permute-start.27) | collective-permute-done | bytes 262176 | tf_op jit(solution)/shard_map/ppermute | solution.py:287
  298.2 6.7 %inverse.4.refs_12_ = f32[32,256,256]{2,1,0:T(8,128)} custom-call(s32[2]{0:T(128)} %pad_add_fusion.half_ref, f32[16,8,8,256]{3,2,1,0:T(8,128)} %copy-done, f32[16,8,8,256]{3,2,1,0:T(8,128)} %copy-done.3, bf16[256,256]{1,0:T(8,128)(2,1)} %constant.45.clone.refs_2_.refs_8_, bf16[256,256]{1,0:T(8,128)(2,1)} %constant.46.clone.refs_3_.refs_9_, ...), custom_call_target="tpu_custom_call" | custom-call | flops 1610612736 | bytes 4194304 | tf_op jit(solution)/shard_map/inverse/pallas_call | solution.py:258
  310.6 6.8 %inverse.5.refs_12_ = f32[32,256,256]{2,1,0:T(8,128)} custom-call(s32[2]{0:T(128)} %pad_add_fusion.half_ref, f32[4,8,8,256]{3,2,1,0:T(8,128)} %get-tuple-element.108.refs_0_, f32[4,8,8,256]{3,2,1,0:T(8,128)} %copy-done.4, f32[4,8,8,256]{3,2,1,0:T(8,128)} %copy-done.5, f32[4,8,8,256]{3,2,1,0:T(8,128)} %copy-done.6, ...), custom_call_target="tpu_custom_call", output_to_operand_aliasing={{}: (13, {})} | custom-call | flops 1610612736 | bytes 4194304 | tf_op jit(solution)/shard_map/inverse/pallas_call | solution.py:258
  317.4 6.8 %inverse.6.refs_12_ = f32[32,256,256]{2,1,0:T(8,128)} custom-call(s32[2]{0:T(128)} %pad_add_fusion.half_ref, f32[4,8,8,256]{3,2,1,0:T(8,128)} %get-tuple-element.100.refs_0_, f32[4,8,8,256]{3,2,1,0:T(8,128)} %copy-done.8, f32[4,8,8,256]{3,2,1,0:T(8,128)} %collective-permute-done.36.refs_2_, ...), custom_call_target="tpu_custom_call", output_to_operand_aliasing={{}: (13, {})} | custom-call | flops 1610612736 | bytes 4194304 | tf_op jit(solution)/shard_map/inverse/pallas_call | solution.py:258
  326.1 5.6 %collective-permute-done.30.refs_6_ = f32[4,8,8,256]{3,2,1,0:T(8,128)S(1)} collective-permute-done((f32[4,8,8,256]{3,2,1,0:T(8,128)}, f32[4,8,8,256]{3,2,1,0:T(8,128)S(1)}, u32[]{:S(2)}, u32[]{:S(2)}) %collective-permute-start.30) | collective-permute-done | bytes 262176 | tf_op jit(solution)/shard_map/ppermute | solution.py:282
  331.7 5.6 %collective-permute-done.31.refs_7_ = f32[4,8,8,256]{3,2,1,0:T(8,128)S(1)} collective-permute-done((f32[4,8,8,256]{3,2,1,0:T(8,128)}, f32[4,8,8,256]{3,2,1,0:T(8,128)S(1)}, u32[]{:S(2)}, u32[]{:S(2)}) %collective-permute-start.31) | collective-permute-done | bytes 262176 | tf_op jit(solution)/shard_map/ppermute | solution.py:282
  338.1 6.8 %inverse.7 = f32[32,256,256]{2,1,0:T(8,128)} custom-call(s32[2]{0:T(128)} %pad_add_fusion.half_ref, f32[4,8,8,256]{3,2,1,0:T(8,128)} %get-tuple-element.92.refs_0_, f32[4,8,8,256]{3,2,1,0:T(8,128)} %copy-done.9, f32[4,8,8,256]{3,2,1,0:T(8,128)} %copy-done.10, f32[4,8,8,256]{3,2,1,0:T(8,128)} %copy-done.11, ...), custom_call_target="tpu_custom_call", output_to_operand_aliasing={{}: (13, {})} | custom-call | flops 1610612736 | bytes 4194304 | tf_op jit(solution)/shard_map/inverse/pallas_call | solution.py:258
  (189 shorter events, 91.9 us)
Async XLA Ops:
  9.6 29.9 %collective-permute-start.21 = (f32[16,8,8,256]{3,2,1,0:T(8,128)}, f32[16,8,8,256]{3,2,1,0:T(8,128)}, u32[]{:S(2)}, u32[]{:S(2)}) collective-permute-start(f32[16,8,8,256]{3,2,1,0:T(8,128)} %get-tuple-element.82), channel_id=1, source_target_pairs={{0,16},{16,0},{1,17},{17,1},{2,18},{18,2},{3,19},{19,3},{4,20},{20... | collective-permute-start | bytes 3145736 | tf_op jit(solution)/shard_map/ppermute | solution.py:282
  19.8 36.6 %collective-permute-start.7 = (f32[16,8,8,256]{3,2,1,0:T(8,128)}, f32[16,8,8,256]{3,2,1,0:T(8,128)}, u32[]{:S(2)}, u32[]{:S(2)}) collective-permute-start(f32[16,8,8,256]{3,2,1,0:T(8,128)} %get-tuple-element.67), channel_id=1, source_target_pairs={{0,16},{16,0},{1,17},{17,1},{2,18},{18,2},{3,19},{19,3},{4,20},{20... | collective-permute-start | bytes 3145736 | tf_op jit(solution)/shard_map/ppermute | solution.py:282
  29.0 49.9 %collective-permute-start = (f32[16,8,8,256]{3,2,1,0:T(8,128)}, f32[16,8,8,256]{3,2,1,0:T(8,128)}, u32[]{:S(2)}, u32[]{:S(2)}) collective-permute-start(f32[16,8,8,256]{3,2,1,0:T(8,128)} %get-tuple-element.61), channel_id=1, source_target_pairs={{0,16},{16,0},{1,17},{17,1},{2,18},{18,2},{3,19},{19,3},{4,20},{20... | collective-permute-start | bytes 3145736 | tf_op jit(solution)/shard_map/ppermute | solution.py:282
  39.2 62.0 %collective-permute-start.14 = (f32[16,8,8,256]{3,2,1,0:T(8,128)}, f32[16,8,8,256]{3,2,1,0:T(8,128)S(1)}, u32[]{:S(2)}, u32[]{:S(2)}) collective-permute-start(f32[16,8,8,256]{3,2,1,0:T(8,128)} %get-tuple-element.76), channel_id=1, source_target_pairs={{0,16},{16,0},{1,17},{17,1},{2,18},{18,2},{3,19},{19,3},{4,20},{20... | collective-permute-start | bytes 3145736 | tf_op jit(solution)/shard_map/ppermute | solution.py:282
  42.4 124.7 %all-to-all-start = ((f32[16,8,8,256]{3,2,1,0:T(8,128)}), f32[16,8,8,256]{3,2,1,0:T(8,128)}, u32[]{:S(2)}, u32[]{:S(2)}) async-start(f32[16,8,8,256]{3,2,1,0:T(8,128)} %add.84), calls=%async_computation | async-start | bytes 2097152 | tf_op jit(solution)/shard_map/all_to_all | solution.py:318
  58.8 44.8 %collective-permute-start.10 = (f32[4,8,8,256]{3,2,1,0:T(8,128)S(1)}, f32[4,8,8,256]{3,2,1,0:T(8,128)S(1)}, u32[]{:S(2)}, u32[]{:S(2)}) collective-permute-start(f32[4,8,8,256]{3,2,1,0:T(8,128)S(1)} %get-tuple-element.117), channel_id=1, source_target_pairs={{0,12},{1,13},{2,14},{3,15},{4,8},{5,9},{6,10},{7,11},{8,4},{9,5},... | collective-permute-start | bytes 786440 | tf_op jit(solution)/shard_map/ppermute | solution.py:287
  60.1 44.5 %collective-permute-start.9 = (f32[4,8,8,256]{3,2,1,0:T(8,128)S(1)}, f32[4,8,8,256]{3,2,1,0:T(8,128)S(1)}, u32[]{:S(2)}, u32[]{:S(2)}) collective-permute-start(f32[4,8,8,256]{3,2,1,0:T(8,128)S(1)} %get-tuple-element.118), channel_id=1, source_target_pairs={{0,8},{1,9},{2,10},{3,11},{4,12},{5,13},{6,14},{7,15},{8,0},{9,1},... | collective-permute-start | bytes 786440 | tf_op jit(solution)/shard_map/ppermute | solution.py:287
  61.1 43.7 %collective-permute-start.8 = (f32[4,8,8,256]{3,2,1,0:T(8,128)S(1)}, f32[4,8,8,256]{3,2,1,0:T(8,128)S(1)}, u32[]{:S(2)}, u32[]{:S(2)}) collective-permute-start(f32[4,8,8,256]{3,2,1,0:T(8,128)S(1)} %get-tuple-element.119), channel_id=1, source_target_pairs={{0,4},{1,5},{2,6},{3,7},{4,0},{5,1},{6,2},{7,3},{8,12},{9,13},{10,... | collective-permute-start | bytes 786440 | tf_op jit(solution)/shard_map/ppermute | solution.py:287
  81.0 32.9 %collective-permute-start.3 = (f32[4,8,8,256]{3,2,1,0:T(8,128)}, f32[4,8,8,256]{3,2,1,0:T(8,128)}, u32[]{:S(2)}, u32[]{:S(2)}) collective-permute-start(f32[4,8,8,256]{3,2,1,0:T(8,128)} %get-tuple-element.121), channel_id=1, source_target_pairs={{0,12},{1,13},{2,14},{3,15},{4,8},{5,9},{6,10},{7,11},{8,4},{9,5},... | collective-permute-start | bytes 786440 | tf_op jit(solution)/shard_map/ppermute | solution.py:287
  101.2 27.3 %collective-permute-start.2 = (f32[4,8,8,256]{3,2,1,0:T(8,128)}, f32[4,8,8,256]{3,2,1,0:T(8,128)}, u32[]{:S(2)}, u32[]{:S(2)}) collective-permute-start(f32[4,8,8,256]{3,2,1,0:T(8,128)} %get-tuple-element.122), channel_id=1, source_target_pairs={{0,8},{1,9},{2,10},{3,11},{4,12},{5,13},{6,14},{7,15},{8,0},{9,1},... | collective-permute-start | bytes 786440 | tf_op jit(solution)/shard_map/ppermute | solution.py:287
  103.6 26.9 %collective-permute-start.1 = (f32[4,8,8,256]{3,2,1,0:T(8,128)S(1)}, f32[4,8,8,256]{3,2,1,0:T(8,128)}, u32[]{:S(2)}, u32[]{:S(2)}) collective-permute-start(f32[4,8,8,256]{3,2,1,0:T(8,128)S(1)} %get-tuple-element.123), channel_id=1, source_target_pairs={{0,4},{1,5},{2,6},{3,7},{4,0},{5,1},{6,2},{7,3},{8,12},{9,13},{10,... | collective-permute-start | bytes 786440 | tf_op jit(solution)/shard_map/ppermute | solution.py:287
  104.6 31.7 %collective-permute-start.17 = (f32[4,8,8,256]{3,2,1,0:T(8,128)S(1)}, f32[4,8,8,256]{3,2,1,0:T(8,128)S(1)}, u32[]{:S(2)}, u32[]{:S(2)}) collective-permute-start(f32[4,8,8,256]{3,2,1,0:T(8,128)S(1)} %get-tuple-element.113), channel_id=1, source_target_pairs={{0,12},{1,13},{2,14},{3,15},{4,8},{5,9},{6,10},{7,11},{8,4},{9,5},... | collective-permute-start | bytes 786440 | tf_op jit(solution)/shard_map/ppermute | solution.py:287
  104.8 35.2 %collective-permute-start.16 = (f32[4,8,8,256]{3,2,1,0:T(8,128)S(1)}, f32[4,8,8,256]{3,2,1,0:T(8,128)S(1)}, u32[]{:S(2)}, u32[]{:S(2)}) collective-permute-start(f32[4,8,8,256]{3,2,1,0:T(8,128)S(1)} %get-tuple-element.114), channel_id=1, source_target_pairs={{0,8},{1,9},{2,10},{3,11},{4,12},{5,13},{6,14},{7,15},{8,0},{9,1},... | collective-permute-start | bytes 786440 | tf_op jit(solution)/shard_map/ppermute | solution.py:287
  113.9 27.2 %collective-permute-start.15 = (f32[4,8,8,256]{3,2,1,0:T(8,128)S(1)}, f32[4,8,8,256]{3,2,1,0:T(8,128)S(1)}, u32[]{:S(2)}, u32[]{:S(2)}) collective-permute-start(f32[4,8,8,256]{3,2,1,0:T(8,128)S(1)} %get-tuple-element.115), channel_id=1, source_target_pairs={{0,4},{1,5},{2,6},{3,7},{4,0},{5,1},{6,2},{7,3},{8,12},{9,13},{10,... | collective-permute-start | bytes 786440 | tf_op jit(solution)/shard_map/ppermute | solution.py:287
  146.5 20.5 %collective-permute-start.20 = (f32[4,8,8,256]{3,2,1,0:T(8,128)}, f32[4,8,8,256]{3,2,1,0:T(8,128)S(1)}, u32[]{:S(2)}, u32[]{:S(2)}) collective-permute-start(f32[4,8,8,256]{3,2,1,0:T(8,128)} %get-tuple-element.80), channel_id=1, source_target_pairs={{0,3},{1,2},{2,1},{3,0},{4,7},{5,6},{6,5},{7,4},{8,11},{9,10},{10,... | collective-permute-start | bytes 786440 | tf_op jit(solution)/shard_map/ppermute | solution.py:287
  177.5 38.7 %all-to-all-start.1 = ((f32[16,8,8,256]{3,2,1,0:T(8,128)}), f32[16,8,8,256]{3,2,1,0:T(8,128)S(1)}, u32[]{:S(2)}, u32[]{:S(2)}) async-start(f32[16,8,8,256]{3,2,1,0:T(8,128)} %get-tuple-element.112), calls=%async_computation.1 | async-start | bytes 2097152 | tf_op jit(solution)/shard_map/all_to_all | solution.py:318
  191.7 19.8 %collective-permute-start.44 = (f32[4,8,8,256]{3,2,1,0:T(8,128)}, f32[4,8,8,256]{3,2,1,0:T(8,128)S(1)}, u32[]{:S(2)}, u32[]{:S(2)}) collective-permute-start(f32[4,8,8,256]{3,2,1,0:T(8,128)} %get-tuple-element.107), channel_id=1, source_target_pairs={{0,3},{1,2},{2,1},{3,0},{4,7},{5,6},{6,5},{7,4},{8,11},{9,10},{10,... | collective-permute-start | bytes 786440 | tf_op jit(solution)/shard_map/ppermute | solution.py:287
  212.2 21.4 %collective-permute-start.24 = (f32[4,8,8,256]{3,2,1,0:T(8,128)}, f32[4,8,8,256]{3,2,1,0:T(8,128)S(1)}, u32[]{:S(2)}, u32[]{:S(2)}) collective-permute-start(f32[4,8,8,256]{3,2,1,0:T(8,128)} %get-tuple-element.91), channel_id=1, source_target_pairs={{0,3},{1,2},{2,1},{3,0},{4,7},{5,6},{6,5},{7,4},{8,11},{9,10},{10,... | collective-permute-start | bytes 786440 | tf_op jit(solution)/shard_map/ppermute | solution.py:287
  216.2 80.6 %collective-permute-start.52 = (f32[16,8,8,256]{3,2,1,0:T(8,128)S(1)}, f32[16,8,8,256]{3,2,1,0:T(8,128)S(1)}, u32[]{:S(2)}, u32[]{:S(2)}) collective-permute-start(f32[16,8,8,256]{3,2,1,0:T(8,128)S(1)} %all-to-all-done.1.refs_0_), channel_id=1, source_target_pairs={{0,16},{16,0},{1,17},{17,1},{2,18},{18,2},{3,19},{19,3},{4,20},{20... | collective-permute-start | bytes 3145736 | tf_op jit(solution)/shard_map/ppermute | solution.py:282
  228.2 33.4 %collective-permute-start.47 = (f32[4,8,8,256]{3,2,1,0:T(8,128)}, f32[4,8,8,256]{3,2,1,0:T(8,128)S(1)}, u32[]{:S(2)}, u32[]{:S(2)}) collective-permute-start(f32[4,8,8,256]{3,2,1,0:T(8,128)} %get-tuple-element.111), channel_id=1, source_target_pairs={{0,12},{1,13},{2,14},{3,15},{4,8},{5,9},{6,10},{7,11},{8,4},{9,5},... | collective-permute-start | bytes 786440 | tf_op jit(solution)/shard_map/ppermute | solution.py:287
  234.3 27.2 %collective-permute-start.48 = (f32[4,8,8,256]{3,2,1,0:T(8,128)}, f32[4,8,8,256]{3,2,1,0:T(8,128)S(1)}, u32[]{:S(2)}, u32[]{:S(2)}) collective-permute-start(f32[4,8,8,256]{3,2,1,0:T(8,128)} %get-tuple-element.108.refs_0_), channel_id=1, source_target_pairs={{0,16},{16,0},{1,17},{17,1},{2,18},{18,2},{3,19},{19,3},{4,20},{20... | collective-permute-start | bytes 786440 | tf_op jit(solution)/shard_map/ppermute | solution.py:282
  237.7 27.2 %collective-permute-start.35 = (f32[4,8,8,256]{3,2,1,0:T(8,128)}, f32[4,8,8,256]{3,2,1,0:T(8,128)S(1)}, u32[]{:S(2)}, u32[]{:S(2)}) collective-permute-start(f32[4,8,8,256]{3,2,1,0:T(8,128)} %get-tuple-element.101), channel_id=1, source_target_pairs={{0,4},{1,5},{2,6},{3,7},{4,0},{5,1},{6,2},{7,3},{8,12},{9,13},{10,... | collective-permute-start | bytes 786440 | tf_op jit(solution)/shard_map/ppermute | solution.py:287
  237.9 27.2 %collective-permute-start.36 = (f32[4,8,8,256]{3,2,1,0:T(8,128)}, f32[4,8,8,256]{3,2,1,0:T(8,128)}, u32[]{:S(2)}, u32[]{:S(2)}) collective-permute-start(f32[4,8,8,256]{3,2,1,0:T(8,128)} %get-tuple-element.102), channel_id=1, source_target_pairs={{0,8},{1,9},{2,10},{3,11},{4,12},{5,13},{6,14},{7,15},{8,0},{9,1},... | collective-permute-start | bytes 786440 | tf_op jit(solution)/shard_map/ppermute | solution.py:287
  265.0 22.1 %collective-permute-start.26 = (f32[4,8,8,256]{3,2,1,0:T(8,128)}, f32[4,8,8,256]{3,2,1,0:T(8,128)S(1)}, u32[]{:S(2)}, u32[]{:S(2)}) collective-permute-start(f32[4,8,8,256]{3,2,1,0:T(8,128)} %get-tuple-element.94), channel_id=1, source_target_pairs={{0,8},{1,9},{2,10},{3,11},{4,12},{5,13},{6,14},{7,15},{8,0},{9,1},... | collective-permute-start | bytes 786440 | tf_op jit(solution)/shard_map/ppermute | solution.py:287
  272.8 22.5 %collective-permute-start.27 = (f32[4,8,8,256]{3,2,1,0:T(8,128)}, f32[4,8,8,256]{3,2,1,0:T(8,128)S(1)}, u32[]{:S(2)}, u32[]{:S(2)}) collective-permute-start(f32[4,8,8,256]{3,2,1,0:T(8,128)} %get-tuple-element.95), channel_id=1, source_target_pairs={{0,12},{1,13},{2,14},{3,15},{4,8},{5,9},{6,10},{7,11},{8,4},{9,5},... | collective-permute-start | bytes 786440 | tf_op jit(solution)/shard_map/ppermute | solution.py:287
  272.9 23.6 %collective-permute-start.49 = (f32[4,8,8,256]{3,2,1,0:T(8,128)S(1)}, f32[4,8,8,256]{3,2,1,0:T(8,128)S(1)}, u32[]{:S(2)}, u32[]{:S(2)}) collective-permute-start(f32[4,8,8,256]{3,2,1,0:T(8,128)S(1)} %collective-permute-done.45.refs_1_), channel_id=1, source_target_pairs={{0,16},{16,0},{1,17},{17,1},{2,18},{18,2},{3,19},{19,3},{4,20},{20... | collective-permute-start | bytes 786440 | tf_op jit(solution)/shard_map/ppermute | solution.py:282
  274.9 30.0 %collective-permute-start.50 = (f32[4,8,8,256]{3,2,1,0:T(8,128)S(1)}, f32[4,8,8,256]{3,2,1,0:T(8,128)}, u32[]{:S(2)}, u32[]{:S(2)}) collective-permute-start(f32[4,8,8,256]{3,2,1,0:T(8,128)S(1)} %collective-permute-done.46.refs_2_), channel_id=1, source_target_pairs={{0,16},{16,0},{1,17},{17,1},{2,18},{18,2},{3,19},{19,3},{4,20},{20... | collective-permute-start | bytes 786440 | tf_op jit(solution)/shard_map/ppermute | solution.py:282
  297.2 20.2 %collective-permute-start.41 = (f32[4,8,8,256]{3,2,1,0:T(8,128)}, f32[4,8,8,256]{3,2,1,0:T(8,128)}, u32[]{:S(2)}, u32[]{:S(2)}) collective-permute-start(f32[4,8,8,256]{3,2,1,0:T(8,128)} %collective-permute-done.37.refs_3_), channel_id=1, source_target_pairs={{0,16},{16,0},{1,17},{17,1},{2,18},{18,2},{3,19},{19,3},{4,20},{20... | collective-permute-start | bytes 786440 | tf_op jit(solution)/shard_map/ppermute | solution.py:282
  304.9 19.3 %collective-permute-start.28 = (f32[4,8,8,256]{3,2,1,0:T(8,128)}, f32[4,8,8,256]{3,2,1,0:T(8,128)S(1)}, u32[]{:S(2)}, u32[]{:S(2)}) collective-permute-start(f32[4,8,8,256]{3,2,1,0:T(8,128)} %get-tuple-element.92.refs_0_), channel_id=1, source_target_pairs={{0,16},{16,0},{1,17},{17,1},{2,18},{18,2},{3,19},{19,3},{4,20},{20... | collective-permute-start | bytes 786440 | tf_op jit(solution)/shard_map/ppermute | solution.py:282
  305.7 20.4 %collective-permute-start.29 = (f32[4,8,8,256]{3,2,1,0:T(8,128)}, f32[4,8,8,256]{3,2,1,0:T(8,128)S(1)}, u32[]{:S(2)}, u32[]{:S(2)}) collective-permute-start(f32[4,8,8,256]{3,2,1,0:T(8,128)} %copy-done.9), channel_id=1, source_target_pairs={{0,16},{16,0},{1,17},{17,1},{2,18},{18,2},{3,19},{19,3},{4,20},{20... | collective-permute-start | bytes 786440 | tf_op jit(solution)/shard_map/ppermute | solution.py:282
  306.4 25.3 %collective-permute-start.30 = (f32[4,8,8,256]{3,2,1,0:T(8,128)}, f32[4,8,8,256]{3,2,1,0:T(8,128)S(1)}, u32[]{:S(2)}, u32[]{:S(2)}) collective-permute-start(f32[4,8,8,256]{3,2,1,0:T(8,128)} %copy-done.10), channel_id=1, source_target_pairs={{0,16},{16,0},{1,17},{17,1},{2,18},{18,2},{3,19},{19,3},{4,20},{20... | collective-permute-start | bytes 786440 | tf_op jit(solution)/shard_map/ppermute | solution.py:282
  309.4 28.0 %collective-permute-start.31 = (f32[4,8,8,256]{3,2,1,0:T(8,128)}, f32[4,8,8,256]{3,2,1,0:T(8,128)S(1)}, u32[]{:S(2)}, u32[]{:S(2)}) collective-permute-start(f32[4,8,8,256]{3,2,1,0:T(8,128)} %copy-done.11), channel_id=1, source_target_pairs={{0,16},{16,0},{1,17},{17,1},{2,18},{18,2},{3,19},{19,3},{4,20},{20... | collective-permute-start | bytes 786440 | tf_op jit(solution)/shard_map/ppermute | solution.py:282
  (64 other events, 1099.6 us)
